TPU v7x, 256 devices: a whole 4x4x8 slice. The times are simulated.
256 devices in a mesh: section: 16 (over z, core), board: 16 (over y, x).
Axes of the slice: x: 4, y: 4, z: 8, core: 2. Of those that a mesh axis runs over, the one named last changes fastest.
Arguments:
- root_reach: float32 [2, 8, 1326], replicated, may hold values from 0.05 to 1
- frontier_value: float32 [2, 8, 1326], replicated, may hold values from -60 to 60
- regret_stop: float32 [16, 64, 8, 1326], P('section', 'board'), may hold values from 1 to 30
- regret_go: float32 [16, 64, 8, 1326], P('section', 'board'), may hold values from 1 to 30
- board_live: int32 [64], P('board'), may hold values from 0 to 1, as said below
- board_cards: int32 [64, 5], P('board'), may hold values from 0 to 51, as said below
- hand_rank: int32 [64, 1326], P('board'), may hold values from 0 to 1325
Outputs:
- new_stop: float32 [16, 64, 8, 1326], P('section', 'board')
- new_go: float32 [16, 64, 8, 1326], P('section', 'board')
- section_values: float32 [16, 2, 8, 1326], P('section')
Inputs may be any that keep to these rules, and one draw needn't show every extreme that they name: `board_live`: 0 or 1; among each device's 4 slots the first one is always 1. `board_cards`: a slot's 5 cards are distinct. `hand_rank`: equal values tie.
All inputs are finite; a program needn't handle non-finite values.
Results may differ from a plain program's by a relative error of at most 0.0008.
Values sent between devices are 32-bit elements; how exact they have to be, the bound alone decides.
A program may use at most 64 MiB of HBM per device.

v0:
```python
import jax
import jax.numpy as jnp
import numpy as np
from jax import lax
from jax.sharding import Mesh
from jax.sharding import PartitionSpec as P

CARDS = 52
SECTION = ("section_0", "section_1")


def neutral_like(value, identity):
    return jax.tree.map(
        lambda a, e: jnp.broadcast_to(jnp.asarray(e, a.dtype), a.shape), value, identity
    )


def prefix_by_axis(value, axes, combine, identity, reverse):
    before = start = neutral_like(value, identity)
    total = value
    for axis in reversed(axes):
        devices, mine = (lax.axis_size(axis), lax.axis_index(axis))
        pieces = jax.tree.map(lambda part: lax.all_gather(part, axis), total)
        inside, total = (start, start)
        for k in reversed(range(devices)) if reverse else range(devices):
            passed = k > mine if reverse else k < mine
            total = combine(total, jax.tree.map(lambda part: part[k], pieces))
            inside = jax.tree.map(lambda new, old: jnp.where(passed, new, old), total, inside)
        before = combine(inside, before)
    return before


def from_everyone(value, axis):
    copies = jnp.broadcast_to(value, (lax.axis_size(axis), *value.shape))
    return lax.all_to_all(copies, axis, split_axis=0, concat_axis=0, tiled=True)


def of_everyone(value, axis):
    everything = from_everyone(value, axis)
    return jnp.sum(everything, axis=0)


def free_pairs():
    first, second = np.triu_indices(CARDS, 1)
    first = jnp.asarray(first.astype(np.int32))
    second = jnp.asarray(second.astype(np.int32))
    shared = (
        (first[:, None] == first[None, :])
        | (first[:, None] == second[None, :])
        | (second[:, None] == first[None, :])
        | (second[:, None] == second[None, :])
    )
    return jnp.where(shared, 0.0, 1.0).astype(jnp.bfloat16)


def board_masks(board_cards):
    first, second = np.triu_indices(CARDS, 1)
    first = jnp.asarray(first.astype(np.int32))
    second = jnp.asarray(second.astype(np.int32))
    hits = (board_cards[:, :, None] == first[None, None, :]) | (
        board_cards[:, :, None] == second[None, None, :]
    )
    return jnp.where(jnp.any(hits, axis=1), 0.0, 1.0).astype(jnp.float32)


def showdown(reach_one, stop_weight, mask_row, rank_row, disjoint):
    leaf_reach = (reach_one * stop_weight).astype(jnp.bfloat16)
    mask_half = mask_row.astype(jnp.bfloat16)
    payoff = (
        jnp.sign(rank_row[:, None] - rank_row[None, :]).astype(jnp.bfloat16)
        * disjoint
        * mask_half[:, None]
        * mask_half[None, :]
    )
    flipped = leaf_reach[::-1].reshape(-1, leaf_reach.shape[-1])
    result = jnp.einsum("rk,hk->rh", flipped, payoff, preferred_element_type=jnp.float32)
    return result.reshape(leaf_reach.shape)


def combine_product(earlier, later):
    return earlier * later


def combine_affine(earlier, later):
    return (later[0] * earlier[0], later[1] + later[0] * earlier[1])


def local(root_reach, frontier_value, regret_stop, regret_go, board_live, board_cards, hand_rank):
    section_idx = lax.axis_index(SECTION)
    players = jnp.arange(2)[:, None, None]
    acting = players == section_idx % 2
    masks = board_masks(board_cards)
    alive = board_live > 0
    alive_weight = alive.astype(jnp.float32)
    stop_now = regret_stop[0]
    go_now = regret_go[0]
    regret_sum = stop_now + go_now
    stop_prob = stop_now / regret_sum
    go_prob = go_now / regret_sum
    factor = jnp.where(acting[None], go_prob[:, None], 1.0)
    stop_weight = jnp.where(acting[None], stop_prob[:, None], 1.0)
    root_masked = root_reach[None] * masks[:, None, None, :]
    before = prefix_by_axis(factor, SECTION, combine_product, jnp.ones_like(factor), False)
    reach_now = root_masked * before
    disjoint = free_pairs()
    leaf_list = []
    for slot in range(masks.shape[0]):
        leaf_one = showdown(
            reach_now[slot], stop_weight[slot], masks[slot], hand_rank[slot], disjoint
        )
        leaf_list.append(leaf_one)
    leaf_values = jnp.stack(leaf_list)
    weighted = stop_weight * leaf_values
    frontier_masked = frontier_value[None] * masks[:, None, None, :]
    lift, offset = prefix_by_axis(
        (factor, weighted),
        SECTION,
        combine_affine,
        (jnp.ones_like(factor), jnp.zeros_like(weighted)),
        True,
    )
    value_next = offset + lift * frontier_masked
    node_value = weighted + factor * value_next
    section_part = jnp.sum(alive_weight[:, None, None, None] * node_value, axis=0)
    live_part = jnp.sum(alive_weight)
    section_sum, live_total = (of_everyone(section_part, "board"), of_everyone(live_part, "board"))
    section_value = section_sum / live_total
    own_next = jnp.sum(jnp.where(acting[None], value_next, 0.0), axis=1)
    own_leaf = jnp.sum(jnp.where(acting[None], leaf_values, 0.0), axis=1)
    gap = own_leaf - own_next
    keep_slot = alive[:, None, None]
    new_stop = jnp.where(keep_slot, jnp.maximum(stop_now + go_prob * gap, 0.0), stop_now)
    new_go = jnp.where(keep_slot, jnp.maximum(go_now - stop_prob * gap, 0.0), go_now)
    return (new_stop[None], new_go[None], section_value[None])


def solution(mesh):
    finer = Mesh(
        mesh.devices.reshape(8, 2, mesh.shape["board"]), ("section_0", "section_1", "board")
    )
    return jax.shard_map(
        local,
        mesh=finer,
        in_specs=(
            P(),
            P(),
            P(SECTION, "board", None, None),
            P(SECTION, "board", None, None),
            P("board"),
            P("board", None),
            P("board", None),
        ),
        out_specs=(
            P(SECTION, "board", None, None),
            P(SECTION, "board", None, None),
            P(SECTION, None, None, None),
        ),
        check_vma=False,
    )
```

profile of v0, /device:TPU:1, one launch (start us, length us, event | category | flops | bytes accessed | tf_op | source)
XLA Modules:
  0.0 157.3 jit_solution(13790962605741336055)
XLA Ops:
  7.2 0.0 all-gather.3.cloned.1.call-start
  7.3 1.0 add_divide_fusion.1
  8.3 0.1 broadcast_select_fusion.1
  8.4 5.1 %all_gather.8 = f32[2,4,2,8,1326]{4,3,2,1,0:T(8,128)S(1)} all-gather(f32[1,4,2,8,1326]{4,3,2,1,0:T(8,128)S(1)} %broadcast_select_fusion.1), channel_id=1, replica_groups=mesh['section_0'=8,'section_1'=2,'board'=16] {'section_1'}, dimensions={0}, use_global_device_ids=true | all-gather | bytes 1018368 | tf_op jit(solution)/shard_map/all_gather | solution.py:23
  13.6 0.8 slice_multiply_fusion
  14.4 0.0 all-gather.5.cloned.1.call-start
  14.5 0.1 copy.15
  14.6 0.1 slice_reduce_fusion.3
  14.7 0.1 or_reduce_fusion
  14.8 0.1 fusion.68
  14.9 0.1 broadcast_select_fusion
  15.0 42.0 %all-gather.3.cloned.1.call-done = f32[8,4,2,8,1326]{4,3,2,1,0:T(8,128)} async-done(((f32[1,4,2,8,1326]{4,3,2,1,0:T(8,128)}), f32[8,4,2,8,1326]{4,3,2,1,0:T(8,128)}) %all-gather.3.cloned.1.call-update) | async-done | bytes 2715664 | tf_op jit(solution)/shard_map/all_gather | solution.py:23
  56.9 2.0 %fusion.48 = f32[4,2,8,1326]{3,2,1,0:T(8,128)S(1)} fusion(f32[8,4,2,8,1326]{4,3,2,1,0:T(8,128)} %all-gather.3.cloned.1.call-done, f32[2,4,2,8,1326]{4,3,2,1,0:T(8,128)S(1)} %all_gather.8, f32[4,1326]{1,0:T(4,128)S(1)} %broadcast_select_fusion.2, f32[2,8,1326]{2,1,0:T(8,128)S(1)} %copy-done.3, pred[]{:T(512)S(6)} %gt.43, pred[]{:T(512)S(6)} %gt.42, ...), kind=kLoop, calls=%fused_computation.74 | loop fusion | flops 1782144 | bytes 3840106 | tf_op jit(solution)/shard_map/mul | solution.py:104
  59.0 3.7 %fusion.16 = f32[2,8,1326]{2,1,0:T(8,128)S(1)} fusion(bf16[2,8,1326]{2,1,0:T(8,128)(2,1)S(1)} %rev.15, s32[1326]{0:T(1024)S(1)} %get-tuple-element.12, s32[1326]{0:T(1024)S(1)} %copy-done.5, s32[1326]{0:T(1024)S(1)} %copy-done.6, bf16[1326]{0:T(1024)(128)(2,1)S(1)} %get-tuple-element.7), kind=kOutput, calls=%fused_computation.21 | convolution fusion | flops 91430352 | bytes 145860 | tf_op jit(solution)/shard_map/rk,hk->rh/dot_general | solution.py:76
  62.7 3.7 %fusion.18 = f32[2,8,1326]{2,1,0:T(8,128)S(1)} fusion(bf16[2,8,1326]{2,1,0:T(8,128)(2,1)S(1)} %rev.14, s32[1326]{0:T(1024)S(1)} %get-tuple-element.13, s32[1326]{0:T(1024)S(1)} %copy-done.5, s32[1326]{0:T(1024)S(1)} %copy-done.6, bf16[1326]{0:T(1024)(128)(2,1)S(1)} %get-tuple-element.8), kind=kOutput, calls=%fused_computation.22 | convolution fusion | flops 91430352 | bytes 145860 | tf_op jit(solution)/shard_map/rk,hk->rh/dot_general | solution.py:76
  66.5 3.7 %fusion.20 = f32[2,8,1326]{2,1,0:T(8,128)S(1)} fusion(bf16[2,8,1326]{2,1,0:T(8,128)(2,1)S(1)} %rev.13, s32[1326]{0:T(1024)S(1)} %get-tuple-element.11, s32[1326]{0:T(1024)S(1)} %copy-done.5, s32[1326]{0:T(1024)S(1)} %copy-done.6, bf16[1326]{0:T(1024)(128)(2,1)S(1)} %get-tuple-element.9), kind=kOutput, calls=%fused_computation.23 | convolution fusion | flops 91430352 | bytes 145860 | tf_op jit(solution)/shard_map/rk,hk->rh/dot_general | solution.py:76
  70.2 3.9 %fusion.22 = f32[2,8,1326]{2,1,0:T(8,128)S(1)} fusion(bf16[2,8,1326]{2,1,0:T(8,128)(2,1)S(1)} %rev.12, s32[1326]{0:T(1024)S(1)} %get-tuple-element.10, s32[1326]{0:T(1024)S(1)} %copy-done.5, s32[1326]{0:T(1024)S(1)} %copy-done.6, bf16[1326]{0:T(1024)(128)(2,1)S(1)} %get-tuple-element.6), kind=kOutput, calls=%fused_computation.24 | convolution fusion | flops 91430352 | bytes 145860 | tf_op jit(solution)/shard_map/rk,hk->rh/dot_general | solution.py:76
  74.1 0.1 maximum_multiply_fusion
  74.2 4.6 %all_gather.10 = f32[2,4,2,8,1326]{4,3,2,1,0:T(8,128)S(1)} all-gather(f32[1,4,2,8,1326]{4,3,2,1,0:T(8,128)S(1)} %maximum_multiply_fusion), channel_id=1, replica_groups=mesh['section_0'=8,'section_1'=2,'board'=16] {'section_1'}, dimensions={0}, use_global_device_ids=true | all-gather | bytes 1018368 | tf_op jit(solution)/shard_map/all_gather | solution.py:23
  78.7 0.8 multiply_add_fusion
  79.6 0.6 convert_reduce_fusion
  80.2 1.2 broadcast_in_dim.139
  81.4 6.4 %all-to-all-start.1 = ((f32[16,1,1]{2,1,0:T(1,128)}), f32[16,1,1]{2,1,0:T(1,128)S(1)}, u32[]{:S(2)}, u32[]{:S(2)}) async-start(f32[16,1,1]{2,1,0:T(1,128)} %broadcast_in_dim.139), calls=%async_computation.1 | async-start | bytes 16384 | tf_op jit(solution)/shard_map/all_to_all | solution.py:35
  87.9 31.5 %all-gather.5.cloned.1.call-done = f32[8,4,2,8,1326]{4,3,2,1,0:T(8,128)} async-done(((f32[1,4,2,8,1326]{4,3,2,1,0:T(8,128)}), f32[8,4,2,8,1326]{4,3,2,1,0:T(8,128)}) %all-gather.5.cloned.1.call-update) | async-done | bytes 2715664 | tf_op jit(solution)/shard_map/all_gather | solution.py:23
  119.4 3.5 %multiply_reduce_fusion = (f32[2,8,1326]{2,1,0:T(8,128)S(1)}, f32[4,8,1326]{2,1,0:T(8,128)S(1)}, f32[4,8,1326]{2,1,0:T(8,128)S(1)}) fusion(f32[1,2,8,1326]{3,2,1,0:T(8,128)S(1)} %bitcast.188, f32[1,2,8,1326]{3,2,1,0:T(8,128)S(1)} %bitcast.190, f32[1,2,8,1326]{3,2,1,0:T(8,128)S(1)} %bitcast.192, f32[1,2,8,1326]{3,2,1,0:T(8,128)S(1)} %bitcast.194, ...), kind=kLoop, calls=%fused_computation.75 | loop fusion | flops 5664672 | bytes 7998460 | tf_op jit(solution)/shard_map/reduce_sum | solution.py:124
  122.9 1.2 broadcast_in_dim.138
  124.1 6.5 %all-to-all-start = ((f32[16,2,8,1326]{3,2,1,0:T(8,128)}), f32[16,2,8,1326]{3,2,1,0:T(8,128)S(1)}, u32[]{:S(2)}, u32[]{:S(2)}) async-start(f32[16,2,8,1326]{3,2,1,0:T(8,128)} %broadcast_in_dim.138), calls=%async_computation | async-start | bytes 2883584 | tf_op jit(solution)/shard_map/all_to_all | solution.py:35
  130.6 0.6 reduce_sum.59
  131.3 0.8 fusion.56
  132.1 17.0 %all-to-all-done = f32[16,2,8,1326]{3,2,1,0:T(8,128)S(1)} async-done(((f32[16,2,8,1326]{3,2,1,0:T(8,128)}), f32[16,2,8,1326]{3,2,1,0:T(8,128)S(1)}, u32[]{:S(2)}, u32[]{:S(2)}) %all-to-all-start) | async-done | bytes 1357856 | tf_op jit(solution)/shard_map/all_to_all | solution.py:35
  149.1 0.1 reduce_sum.57
  149.2 1.3 divide_bitcast_fusion
  (29 shorter events, 0.2 us)
Async XLA Ops:
  7.2 7.5 %copy-start.5 = (s32[1326]{0:T(1024)S(1)}, s32[1326]{0:T(1024)}, u32[]{:S(2)}) copy-start(s32[1326]{0:T(1024)} %constant.52.clone) | copy-start | bytes 15916
  7.2 7.5 %copy-start.6 = (s32[1326]{0:T(1024)S(1)}, s32[1326]{0:T(1024)}, u32[]{:S(2)}) copy-start(s32[1326]{0:T(1024)} %constant.51.clone) | copy-start | bytes 15916
  7.2 7.3 %copy-start.7 = (s32[4,5]{1,0:T(4,128)S(1)}, s32[4,5]{1,0:T(4,128)}, u32[]{:S(2)}) copy-start(s32[4,5]{1,0:T(4,128)} %param.16) | copy-start | bytes 244
  7.2 7.4 %copy-start.4 = (s32[4,1326]{1,0:T(4,128)S(1)}, s32[4,1326]{1,0:T(4,128)}, u32[]{:S(2)}) copy-start(s32[4,1326]{1,0:T(4,128)} %param.17) | copy-start | bytes 63652
  7.2 49.7 %copy-start.3 = (f32[2,8,1326]{2,1,0:T(8,128)S(1)}, f32[2,8,1326]{2,1,0:T(8,128)}, u32[]{:S(2)}) copy-start(f32[2,8,1326]{2,1,0:T(8,128)} %param.11) | copy-start | bytes 254596
  7.2 49.7 %all-gather.3.cloned.1.call-start = ((), (), s32[]{:S(2)}) async-start(), calls=%async_computation.2 | async-start | bytes 3244032 | tf_op jit(solution)/shard_map/all_gather | solution.py:23
  14.4 105.0 %all-gather.5.cloned.1.call-start = ((), (), s32[]{:S(2)}) async-start(), calls=%async_computation.3 | async-start | bytes 3244032 | tf_op jit(solution)/shard_map/all_gather | solution.py:23
  74.1 5.5 %copy-start.8 = (s32[4]{0:T(128)S(1)}, s32[4]{0:T(128)}, u32[]{:S(2)}) copy-start(s32[4]{0:T(128)} %param.15) | copy-start | bytes 52
  74.1 45.4 %copy-start.2 = (f32[2,8,1326]{2,1,0:T(8,128)S(1)}, f32[2,8,1326]{2,1,0:T(8,128)}, u32[]{:S(2)}) copy-start(f32[2,8,1326]{2,1,0:T(8,128)} %param.12) | copy-start | bytes 254596
  81.4 41.5 %all-to-all-start.1 = ((f32[16,1,1]{2,1,0:T(1,128)}), f32[16,1,1]{2,1,0:T(1,128)S(1)}, u32[]{:S(2)}, u32[]{:S(2)}) async-start(f32[16,1,1]{2,1,0:T(1,128)} %broadcast_in_dim.139), calls=%async_computation.1 | async-start | bytes 16384 | tf_op jit(solution)/shard_map/all_to_all | solution.py:35
  122.9 8.4 %copy-start = (f32[1,4,8,1326]{3,2,1,0:T(8,128)S(1)}, f32[1,4,8,1326]{3,2,1,0:T(8,128)}, u32[]{:S(2)}) copy-start(f32[1,4,8,1326]{3,2,1,0:T(8,128)} %param.14) | copy-start | bytes 509188
  122.9 8.4 %copy-start.1 = (f32[1,4,8,1326]{3,2,1,0:T(8,128)S(1)}, f32[1,4,8,1326]{3,2,1,0:T(8,128)}, u32[]{:S(2)}) copy-start(f32[1,4,8,1326]{3,2,1,0:T(8,128)} %param.13) | copy-start | bytes 509188
  124.1 25.0 %all-to-all-start = ((f32[16,2,8,1326]{3,2,1,0:T(8,128)}), f32[16,2,8,1326]{3,2,1,0:T(8,128)S(1)}, u32[]{:S(2)}, u32[]{:S(2)}) async-start(f32[16,2,8,1326]{3,2,1,0:T(8,128)} %broadcast_in_dim.138), calls=%async_computation | async-start | bytes 2883584 | tf_op jit(solution)/shard_map/all_to_all | solution.py:35
Sparse Core Ops, SparseCore 0:
  14.5 42.3 all-gather.2
  79.7 39.6 all-gather.4
where the time goes:
time: 160 us; the launch traced here: 157 us
  waiting for transfers between devices  90.5 us (57%)
  matrix products  15 us (9%)
  between operations  14.3 us (9%)
  starting transfers between devices  13 us (8%)
  other arithmetic  12 us (8%)
  blocking collectives  9.7 us (6%)
  local copies, waits for them, and re-layouts  2.75 us (2%)
    all_gather x2, waiting for transfers between devices, prefix_by_axis(): pieces = jax.tree.map(lambda part: lax.all_gather(part, axis), total)  73.5 us
    all_to_all x2, waiting for transfers between devices, from_everyone(): return lax.all_to_all(copies, axis, split_axis=0, concat_axis=0, tiled=True)  17 us
    dot_general x4, matrix products, showdown(): jnp.einsum('rk,hk->rh', flipped, payoff, preferred_element_type=jnp.float32)  15 us
    all_to_all x2, starting transfers between devices, from_everyone(): return lax.all_to_all(copies, axis, split_axis=0, concat_axis=0, tiled=True)  12.9 us
    all_gather x2, blocking collectives, prefix_by_axis(): pieces = jax.tree.map(lambda part: lax.all_gather(part, axis), total)  9.7 us
    reduce_sum x1, other arithmetic, local(): jnp.sum(alive_weight[:, None, None, None] * node_value, axis=0)  3.47 us
  transfers between devices with their start and end apart: 4, of which 3 were waited for; matrix products, arithmetic and copies ran while one was open for 5% of the time, Pallas kernels for 0%

commit v1 on v0

v1 whole, which is shorter than its diff:
```python
import jax
import jax.numpy as jnp
import numpy as np
from jax import lax
from jax.experimental import pallas as pl
from jax.experimental.pallas import tpu as pltpu
from jax.sharding import PartitionSpec as P

CARDS = 52
H = 1326
NODES = 8
TILES = 11
HP = TILES * 128
LAST = H - 128 * (TILES - 1)
SECTIONS = 16
COLUMNS = 16
BOARD_DEV = 4
ROWS = 24
HALF = 16
MESH = pl.DeviceIdType.MESH


def hand_bits():
    first, second = np.triu_indices(CARDS, 1)
    low = np.full((HP,), -1, np.int64)
    high = np.full((HP,), -1, np.int64)
    both = (np.int64(1) << first) | (np.int64(1) << second)
    low[:H] = both & 0xFFFFFFFF
    high[:H] = both >> 32
    rows = np.stack([low, high]).astype(np.uint32).view(np.int32)
    scan = np.full((2, ROWS, 128), -1, np.int32)
    for word in range(2):
        tiles = rows[word].reshape(TILES, 128)
        scan[word, :TILES] = tiles
        scan[word, TILES : 2 * TILES] = tiles
    return rows, scan.reshape(2 * ROWS, 128)


def remote(src, dst, send, recv, section, board):
    return pltpu.make_async_remote_copy(
        src_ref=src,
        dst_ref=dst,
        send_sem=send,
        recv_sem=recv,
        device_id={"section": section, "board": board},
        device_id_type=MESH,
    )


def slot(ref, index, rows):
    return ref.at[pl.ds(pl.multiple_of(index * rows, 8), rows), :]


def kernel(
    root_hbm, front_hbm, stop_hbm, go_hbm, live_hbm, cards_hbm, rank_hbm, bits_hbm, scan_hbm,
    out_stop, out_go, out_sec,
    root_v, front_v, stop_v, go_v, live_s, cards_s, rank_v, bits_v, scan_v,
    pad, asend, arecv, ends, colrow, cols, bcast, w, lsc, lhs, leafsc,
    gsend, grecv, nsc, rsend, rrecv, fsend, frecv,
    in_sem, a_ss, a_rs, g_ss, g_rs, r_ss, r_rs, f_ss, f_rs,
):
    me = lax.axis_index("section")
    col = lax.axis_index("board")
    node = me // 2
    core = me % 2

    barrier = pltpu.get_barrier_semaphore()
    for d in range(1, SECTIONS):
        pl.semaphore_signal(
            barrier, inc=1, device_id={"section": (me + d) % SECTIONS, "board": col}, device_id_type=MESH
        )
    for dc in range(2):
        for db in range(1, COLUMNS):
            pl.semaphore_signal(
                barrier,
                inc=1,
                device_id={"section": 2 * node + (core + dc) % 2, "board": (col + db) % COLUMNS},
                device_id_type=MESH,
            )

    loads = [
        pltpu.make_async_copy(src, dst, in_sem.at[i])
        for i, (src, dst) in enumerate(
            [
                (stop_hbm, stop_v), (go_hbm, go_v), (root_hbm, root_v), (front_hbm, front_v),
                (live_hbm, live_s), (cards_hbm, cards_s), (rank_hbm, rank_v), (bits_hbm, bits_v),
                (scan_hbm, scan_v),
            ]
        )
    ]
    for copy in loads:
        copy.start()
    pad[...] = jnp.full(pad.shape, 0.5, jnp.float32)
    ends[...] = jnp.zeros(ends.shape, jnp.float32)
    loads[0].wait()
    loads[1].wait()

    for j in range(BOARD_DEV):
        for t in range(TILES):
            if t < TILES - 1:
                at = pl.ds(128 * t, 128)
                tile = go_v[j, :, at] / (go_v[j, :, at] + stop_v[j, :, at])
            else:
                at = pl.ds(128 * t, LAST)
                pad[j, :, :LAST] = go_v[j, :, at] / (go_v[j, :, at] + stop_v[j, :, at])
                tile = pad[j]
            row = (j // 2) * ROWS + (j % 2) * TILES + t
            asend[pl.ds(row, NODES, stride=2 * ROWS), :] = tile
    pl.semaphore_wait(barrier, SECTIONS - 1 + 2 * (COLUMNS - 1))

    def a_copy(to):
        return remote(
            slot(asend, to, ROWS), slot(arecv, me, ROWS), a_ss.at[to], a_rs.at[me], to, col
        )

    order = sorted(range(1, SECTIONS), key=lambda d: -min(d, SECTIONS - d))
    for d in order:
        a_copy((me + d) % SECTIONS).start()
    own = pl.ds(pl.multiple_of(me * ROWS, 8), ROWS)
    arecv[own, :] = asend[own, :]

    for copy in loads[2:]:
        copy.wait()

    alive = []
    board_bits = []
    for jj in range(2):
        j = 2 * core + jj
        alive.append(jnp.where(live_s[j] > 0, 1.0, 0.0).astype(jnp.float32))
        low = jnp.int32(0)
        high = jnp.int32(0)
        for i in range(5):
            card = cards_s[j, i]
            bit = lax.shift_left(jnp.int32(1), card % 32)
            low = low | jnp.where(card < 32, bit, 0)
            high = high | jnp.where(card < 32, 0, bit)
        board_bits.append((low, high))
    row_id = lax.broadcasted_iota(jnp.int32, (ROWS, 128), 0)
    first_slot = row_id < TILES
    low = jnp.where(first_slot, board_bits[0][0], board_bits[1][0])
    high = jnp.where(first_slot, board_bits[0][1], board_bits[1][1])
    hit = (scan_v[:ROWS, :] & low) | (scan_v[ROWS:, :] & high)
    mask = jnp.where(hit == 0, 1.0, 0.0).astype(jnp.float32)
    inside = (scan_v[:ROWS, :] & scan_v[ROWS:, :]) != -1
    alive_rows = jnp.where(first_slot, alive[0], alive[1])

    for which, ref in enumerate((root_v, front_v)):
        for p in range(2):
            base = (2 * which + p) * NODES * ROWS
            pad[p, :, :] = jnp.zeros((NODES, 128), jnp.float32)
            pad[p, :, :LAST] = ref[p, :, pl.ds(128 * (TILES - 1), LAST)]
            for t in range(TILES):
                tile = ref[p, :, pl.ds(128 * t, 128)] if t < TILES - 1 else pad[p]
                ends[pl.ds(base + t, NODES, stride=ROWS), :] = tile
                ends[pl.ds(base + TILES + t, NODES, stride=ROWS), :] = tile

    def end_of(index):
        at = pl.multiple_of((index * NODES + node) * ROWS, 8)
        return jnp.where(mask > 0, ends[pl.ds(at, ROWS), :], 0.0)

    colrow[...] = jnp.zeros(colrow.shape, jnp.int32)
    colrow[0:2, :] = bits_v[...]
    for jj in range(2):
        colrow[2 + jj : 3 + jj, :H] = rank_v[pl.ds(2 * core + jj, 1), :]
    for r in range(4):
        bcast[r] = jnp.broadcast_to(colrow[r : r + 1, :], (8, HP))
    for t in range(TILES):
        cols[128 * t : 128 * (t + 1), :] = colrow[:, 128 * t : 128 * (t + 1)].T

    def payoff_rows(block, _):
        at = pl.multiple_of(block * 16, 16)
        col_of = cols[pl.ds(at, 16), :]
        wide = [jnp.broadcast_to(col_of[:, r : r + 1], (16, 128)) for r in range(4)]
        for t in range(TILES):
            lanes = slice(128 * t, 128 * (t + 1))
            row = [jnp.concatenate([bcast[r, :, lanes]] * 2, axis=0) for r in range(4)]
            free = ((wide[0] & row[0]) | (wide[1] & row[1])) == 0
            for jj in range(2):
                step = jnp.minimum(jnp.maximum(row[2 + jj] - wide[2 + jj], -1), 1)
                w[jj, pl.ds(at, 16), lanes] = jnp.where(free, step, 0).astype(jnp.float32).astype(jnp.bfloat16)
        return 0

    lax.fori_loop(0, HP // 16, payoff_rows, 0)

    for d in range(1, SECTIONS):
        other = (me + d) % SECTIONS
        remote(slot(asend, other, ROWS), slot(arecv, other, ROWS), a_ss.at[other], a_rs.at[other], other, col).wait_recv()

    reach = [end_of(0), end_of(1)]
    for s in range(SECTIONS):
        go = jnp.where(inside, arecv[s * ROWS : (s + 1) * ROWS, :], 0.5)
        q = s % 2
        lsc[q, s * ROWS : (s + 1) * ROWS, :] = reach[q] * (1.0 - go)
        lsc[1 - q, s * ROWS : (s + 1) * ROWS, :] = reach[1 - q]
        reach[q] = reach[q] * go
    for jj in range(2):
        for p in range(2):
            for t in range(TILES):
                tile = lsc[p, pl.ds(jj * TILES + t, SECTIONS, stride=ROWS), :]
                lhs[jj, p * SECTIONS : (p + 1) * SECTIONS, 128 * t : 128 * (t + 1)] = tile.astype(jnp.bfloat16)
    for jj in range(2):
        leaf = jnp.dot(lhs[jj], w[jj], preferred_element_type=jnp.float32)
        for p in range(2):
            for t in range(TILES):
                tile = leaf[p * SECTIONS : (p + 1) * SECTIONS, 128 * t : 128 * (t + 1)]
                leafsc[1 - p, pl.ds(jj * TILES + t, SECTIONS, stride=ROWS), :] = tile

    value = [end_of(2), end_of(3)]
    for s in reversed(range(SECTIONS)):
        q = s % 2
        rows = slice(s * ROWS, (s + 1) * ROWS)
        go = jnp.where(inside, arecv[rows, :], 0.5)
        leaf_q = leafsc[q, rows, :] * mask
        leaf_o = leafsc[1 - q, rows, :] * mask
        gsend[rows, :] = leaf_q - value[q]
        value[q] = (1.0 - go) * leaf_q + go * value[q]
        value[1 - q] = leaf_o + value[1 - q]
        for p in range(2):
            at = (2 * s + p) * ROWS
            nsc[at : at + ROWS, :] = jnp.where(inside, value[p], 1.0) * alive_rows
            half = (2 * s + p) * HALF
            rsend[half : half + TILES, :] = nsc[at : at + TILES, :] + nsc[at + TILES : at + 2 * TILES, :]

    def r_copy(dc, db):
        to_core = (core + dc) % 2
        to_col = (col + db) % COLUMNS
        to = 2 * node + to_core
        s = (to_col + to) % SECTIONS
        return remote(
            slot(rsend, 2 * s + to_core, HALF), rrecv.at[dc * COLUMNS + db], r_ss.at[dc * COLUMNS + db],
            r_rs.at[dc * COLUMNS + db], to, to_col,
        )

    pairs = [(dc, db) for db in range(COLUMNS) for dc in range(2) if dc or db]
    for dc, db in pairs:
        r_copy(dc, db).start()

    def g_copy(to):
        return remote(
            slot(gsend, to, ROWS), slot(grecv, me, ROWS), g_ss.at[to], g_rs.at[me], to, col
        )

    for d in order:
        g_copy((me + d) % SECTIONS).start()
    grecv[own, :] = gsend[own, :]

    mine = (col + me) % SECTIONS
    total = rsend[pl.ds(pl.multiple_of((2 * mine + core) * HALF, 8), HALF), :]
    for dc, db in pairs:
        r_copy(dc, db).wait_recv()
        total = total + rrecv[dc * COLUMNS + db]
    fsend[...] = total / total[TILES - 1 : TILES, 127:128]

    def f_copy(db):
        return remote(fsend, slot(frecv, me, HALF), f_ss.at[db], f_rs.at[me], mine, (col + db) % COLUMNS)

    for db in range(1, COLUMNS):
        f_copy(db).start()

    @pl.when(col != 0)
    def _():
        f_copy(0).start()

    @pl.when(col == 0)
    def _():
        frecv[pl.ds(pl.multiple_of(me * HALF, 8), HALF), :] = fsend[...]

    for d in range(1, SECTIONS):
        other = (me + d) % SECTIONS
        remote(slot(gsend, other, ROWS), slot(grecv, other, ROWS), g_ss.at[other], g_rs.at[other], other, col).wait_recv()
    for j in range(BOARD_DEV):
        keep = live_s[j] > 0
        for t in range(TILES):
            size = 128 if t < TILES - 1 else LAST
            at = pl.ds(128 * t, size)
            gap = grecv[pl.ds((j // 2) * ROWS + (j % 2) * TILES + t, NODES, stride=2 * ROWS), :][:, :size]
            stop = stop_v[j, :, at]
            go = go_v[j, :, at]
            total_regret = stop + go
            out_stop[j, :, at] = jnp.where(keep, jnp.maximum(stop + go / total_regret * gap, 0.0), stop)
            out_go[j, :, at] = jnp.where(keep, jnp.maximum(go - stop / total_regret * gap, 0.0), go)

    for k in range(SECTIONS):
        @pl.when(jnp.logical_or(me != k, col != 0))
        def _(k=k):
            remote(fsend, slot(frecv, k, HALF), f_ss.at[0], f_rs.at[k], mine, col).wait_recv()
    for p in range(2):
        for t in range(TILES):
            size = 128 if t < TILES - 1 else LAST
            tile = frecv[pl.ds(p * HALF + t, NODES, stride=2 * HALF), :]
            out_sec[p, :, pl.ds(128 * t, size)] = tile[:, :size]

    for d in order:
        a_copy((me + d) % SECTIONS).wait_send()
        g_copy((me + d) % SECTIONS).wait_send()
    for dc, db in pairs:
        r_copy(dc, db).wait_send()
    for db in range(1, COLUMNS):
        f_copy(db).wait_send()

    @pl.when(col != 0)
    def _():
        f_copy(0).wait_send()


def local(root_reach, frontier_value, regret_stop, regret_go, board_live, board_cards, hand_rank):
    bits, scan = hand_bits()
    f32, i32 = jnp.float32, jnp.int32
    regrets = (BOARD_DEV, NODES, H)
    ends = (2, NODES, H)
    any_spec = pl.BlockSpec(memory_space=pl.ANY)
    vmem_spec = pl.BlockSpec(memory_space=pltpu.VMEM)
    dma = pltpu.SemaphoreType.DMA
    new_stop, new_go, section_value = pl.pallas_call(
        kernel,
        out_shape=(
            jax.ShapeDtypeStruct(regrets, f32),
            jax.ShapeDtypeStruct(regrets, f32),
            jax.ShapeDtypeStruct(ends, f32),
        ),
        in_specs=[any_spec] * 9,
        out_specs=(vmem_spec,) * 3,
        scratch_shapes=[
            pltpu.VMEM(ends, f32), pltpu.VMEM(ends, f32), pltpu.VMEM(regrets, f32), pltpu.VMEM(regrets, f32),
            pltpu.SMEM((BOARD_DEV,), i32), pltpu.SMEM((BOARD_DEV, 5), i32), pltpu.VMEM((BOARD_DEV, H), i32),
            pltpu.VMEM((2, HP), i32), pltpu.VMEM((2 * ROWS, 128), i32),
            pltpu.VMEM((BOARD_DEV, NODES, 128), f32),
            pltpu.VMEM((SECTIONS * ROWS, 128), f32), pltpu.VMEM((SECTIONS * ROWS, 128), f32),
            pltpu.VMEM((4 * NODES * ROWS, 128), f32),
            pltpu.VMEM((8, HP), i32), pltpu.VMEM((HP, 8), i32), pltpu.VMEM((4, 8, HP), i32),
            pltpu.VMEM((2, HP, HP), jnp.bfloat16),
            pltpu.VMEM((2, SECTIONS * ROWS, 128), f32), pltpu.VMEM((2, 2 * SECTIONS, HP), jnp.bfloat16),
            pltpu.VMEM((2, SECTIONS * ROWS, 128), f32),
            pltpu.VMEM((SECTIONS * ROWS, 128), f32), pltpu.VMEM((SECTIONS * ROWS, 128), f32),
            pltpu.VMEM((2 * SECTIONS * ROWS, 128), f32),
            pltpu.VMEM((2 * SECTIONS * HALF, 128), f32), pltpu.VMEM((2 * COLUMNS, HALF, 128), f32),
            pltpu.VMEM((HALF, 128), f32), pltpu.VMEM((SECTIONS * HALF, 128), f32),
            dma((9,)), dma((SECTIONS,)), dma((SECTIONS,)), dma((SECTIONS,)), dma((SECTIONS,)),
            dma((2 * COLUMNS,)), dma((2 * COLUMNS,)), dma((COLUMNS,)), dma((SECTIONS,)),
        ],
        compiler_params=pltpu.CompilerParams(
            collective_id=0, has_side_effects=True, vmem_limit_bytes=40 * 1024 * 1024
        ),
    )(
        root_reach, frontier_value, regret_stop[0], regret_go[0], board_live, board_cards, hand_rank,
        jnp.asarray(bits), jnp.asarray(scan),
    )
    return new_stop[None], new_go[None], section_value[None]


def solution(mesh):
    regrets = P("section", "board", None, None)
    return jax.shard_map(
        local,
        mesh=mesh,
        in_specs=(P(), P(), regrets, regrets, P("board"), P("board", None), P("board", None)),
        out_specs=(regrets, regrets, P("section", None, None, None)),
        check_vma=False,
    )
```

time: 160 us -> 52.6 us (0.33); the launches traced: 157 us -> 52 us
  waiting for transfers between devices: 90.5 us -> 0 us
  Pallas kernels: 0 us -> 42.9 us
  matrix products: 15 us -> 0 us
  between operations: 14.3 us -> 0.67 us
  starting transfers between devices: 13 us -> 0 us
  other arithmetic: 12 us -> 0 us
  blocking collectives: 9.7 us -> 0 us
  local copies, waits for them, and re-layouts: 2.75 us -> 8.45 us
    all_gather x2 -> x0, waiting for transfers between devices: 73.5 us -> none  [prefix_by_axis(): pieces = jax.tree.map(lambda part: lax.all_gather(part, axis), total)]
    pallas_call x0 -> x1, Pallas kernels: none -> 42.9 us  [local(): pl.pallas_call(kernel, out_shape=(jax.ShapeDtypeStruct(regrets, f32), jax...]
    all_to_all x2 -> x0, waiting for transfers between devices: 17 us -> none  [from_everyone(): return lax.all_to_all(copies, axis, split_axis=0, concat_axis=0, tiled=True)]
    dot_general x4 -> x0, matrix products: 15 us -> none  [showdown(): jnp.einsum('rk,hk->rh', flipped, payoff, preferred_element_type=jnp.float32)]
    all_to_all x2 -> x0, starting transfers between devices: 12.9 us -> none  [from_everyone(): return lax.all_to_all(copies, axis, split_axis=0, concat_axis=0, tiled=True)]
    all_gather x2 -> x0, blocking collectives: 9.7 us -> none  [prefix_by_axis(): pieces = jax.tree.map(lambda part: lax.all_gather(part, axis), total)]
    unnamed x19 -> x21, local copies, waits for them, and re-layouts: 0.14 us -> 8.45 us
    reduce_sum x4 -> x0, other arithmetic: 4.78 us -> none  [the longest x1 3.47 us: local(): jnp.sum(alive_weight[:, None, None, None] * node_value, axis=0)]
  transfers between devices with their start and end apart: 4 -> 0, of which waited for: 3 -> 0; matrix products, arithmetic and copies ran while one was open for 5% -> 0% of each run, Pallas kernels for 0% -> 0%
where the time goes in v1:
time: 52.6 us; the launch traced here: 52 us
  Pallas kernels  42.9 us (82%)
  local copies, waits for them, and re-layouts  8.45 us (16%)
  between operations  0.67 us (1%)
    pallas_call x1, Pallas kernels, local(): pl.pallas_call(kernel, out_shape=(jax.ShapeDtypeStruct(regrets, f32), jax...  42.9 us
    unnamed x21, local copies, waits for them, and re-layouts  8.45 us

profile of v1, /device:TPU:1, one launch (start us, length us, event | category | flops | bytes accessed | tf_op | source)
XLA Modules:
  0.0 52.0 jit_solution(4804775293821948974)
XLA Ops:
  0.6 0.0 copy-start.7
  0.6 0.0 copy-start.8
  0.7 0.7 %copy-done.7 = s32[4,5]{1,0:T(4,128)S(1)} copy-done((s32[4,5]{1,0:T(4,128)S(1)}, s32[4,5]{1,0:T(4,128)}, u32[]{:S(2)}) %copy-start.7) | copy-done | bytes 104
  1.3 0.0 copy-done.8
  1.3 0.0 copy-start
  1.3 0.9 %copy-done = f32[1,4,8,1326]{3,2,1,0:T(8,128)S(1)} copy-done((f32[1,4,8,1326]{3,2,1,0:T(8,128)S(1)}, f32[1,4,8,1326]{3,2,1,0:T(8,128)}, u32[]{:S(2)}) %copy-start) | copy-done | bytes 169752
  2.2 0.0 copy-start.1
  2.2 0.9 %copy-done.1 = f32[1,4,8,1326]{3,2,1,0:T(8,128)S(1)} copy-done((f32[1,4,8,1326]{3,2,1,0:T(8,128)S(1)}, f32[1,4,8,1326]{3,2,1,0:T(8,128)}, u32[]{:S(2)}) %copy-start.1) | copy-done | bytes 169752
  3.2 0.0 copy-start.2
  3.2 0.9 %copy-done.2 = f32[2,8,1326]{2,1,0:T(8,128)S(1)} copy-done((f32[2,8,1326]{2,1,0:T(8,128)S(1)}, f32[2,8,1326]{2,1,0:T(8,128)}, u32[]{:S(2)}) %copy-start.2) | copy-done | bytes 84888
  4.1 0.0 copy-start.3
  4.1 0.9 %copy-done.3 = f32[2,8,1326]{2,1,0:T(8,128)S(1)} copy-done((f32[2,8,1326]{2,1,0:T(8,128)S(1)}, f32[2,8,1326]{2,1,0:T(8,128)}, u32[]{:S(2)}) %copy-start.3) | copy-done | bytes 84888
  4.9 0.0 copy-start.4
  4.9 0.7 %copy-done.4 = s32[48,128]{1,0:T(8,128)S(1)} copy-done((s32[48,128]{1,0:T(8,128)S(1)}, s32[48,128]{1,0:T(8,128)}, u32[]{:S(2)}) %copy-start.4) | copy-done | bytes 24600
  5.7 0.0 copy-start.5
  5.7 0.7 %copy-done.5 = s32[4,1326]{1,0:T(4,128)S(1)} copy-done((s32[4,1326]{1,0:T(4,128)S(1)}, s32[4,1326]{1,0:T(4,128)}, u32[]{:S(2)}) %copy-start.5) | copy-done | bytes 21240
  6.4 0.0 copy-start.6
  6.4 0.7 %copy-done.6 = s32[2,1408]{1,0:T(2,128)S(1)} copy-done((s32[2,1408]{1,0:T(2,128)S(1)}, s32[2,1408]{1,0:T(2,128)}, u32[]{:S(2)}) %copy-start.6) | copy-done | bytes 11288
  7.1 42.9 %shard_map.112 = (f32[4,8,1326]{2,1,0:T(8,128)S(1)}, f32[4,8,1326]{2,1,0:T(8,128)S(1)}, f32[2,8,1326]{2,1,0:T(8,128)S(1)}) custom-call(f32[2,8,1326]{2,1,0:T(8,128)S(1)} %copy-done.2, f32[2,8,1326]{2,1,0:T(8,128)S(1)} %copy-done.3, f32[4,8,1326]{2,1,0:T(8,128)S(1)} %bitcast.7, f32[4,8,1326]{2,1,0:T(8,128)S(1)} %bitcast.8, s32[4]{0:T(128)S(1)} %copy-done.8, ...), custom_call_target="tpu_custom_call" | custom-call | tf_op jit(solution)/shard_map/pallas_call | solution.py:314
  50.0 0.7 %copy.15 = f32[1,4,8,1326]{3,2,1,0:T(8,128)} copy(f32[1,4,8,1326]{3,2,1,0:T(8,128)S(1)} %bitcast.6) | data formatting | bytes 339456
  50.7 0.7 %copy.16 = f32[1,4,8,1326]{3,2,1,0:T(8,128)} copy(f32[1,4,8,1326]{3,2,1,0:T(8,128)S(1)} %bitcast.5) | data formatting | bytes 339456
  51.4 0.6 %copy.17 = f32[1,2,8,1326]{3,2,1,0:T(8,128)} copy(f32[1,2,8,1326]{3,2,1,0:T(8,128)S(1)} %bitcast.9) | data formatting | bytes 169728
Async XLA Ops:
  0.6 0.7 %copy-start.7 = (s32[4,5]{1,0:T(4,128)S(1)}, s32[4,5]{1,0:T(4,128)}, u32[]{:S(2)}) copy-start(s32[4,5]{1,0:T(4,128)} %cards_hbm.1) | copy-start | bytes 244
  0.6 0.7 %copy-start.8 = (s32[4]{0:T(128)S(1)}, s32[4]{0:T(128)}, u32[]{:S(2)}) copy-start(s32[4]{0:T(128)} %live_hbm.1) | copy-start | bytes 52
  1.3 0.9 %copy-start = (f32[1,4,8,1326]{3,2,1,0:T(8,128)S(1)}, f32[1,4,8,1326]{3,2,1,0:T(8,128)}, u32[]{:S(2)}) copy-start(f32[1,4,8,1326]{3,2,1,0:T(8,128)} %param.11) | copy-start | bytes 509188
  2.2 0.9 %copy-start.1 = (f32[1,4,8,1326]{3,2,1,0:T(8,128)S(1)}, f32[1,4,8,1326]{3,2,1,0:T(8,128)}, u32[]{:S(2)}) copy-start(f32[1,4,8,1326]{3,2,1,0:T(8,128)} %param.12) | copy-start | bytes 509188
  3.2 0.9 %copy-start.2 = (f32[2,8,1326]{2,1,0:T(8,128)S(1)}, f32[2,8,1326]{2,1,0:T(8,128)}, u32[]{:S(2)}) copy-start(f32[2,8,1326]{2,1,0:T(8,128)} %root_hbm.1) | copy-start | bytes 254596
  4.1 0.9 %copy-start.3 = (f32[2,8,1326]{2,1,0:T(8,128)S(1)}, f32[2,8,1326]{2,1,0:T(8,128)}, u32[]{:S(2)}) copy-start(f32[2,8,1326]{2,1,0:T(8,128)} %front_hbm.1) | copy-start | bytes 254596
  4.9 0.7 %copy-start.4 = (s32[48,128]{1,0:T(8,128)S(1)}, s32[48,128]{1,0:T(8,128)}, u32[]{:S(2)}) copy-start(s32[48,128]{1,0:T(8,128)} %constant.5.clone.scan_hbm) | copy-start | bytes 73732
  5.7 0.7 %copy-start.5 = (s32[4,1326]{1,0:T(4,128)S(1)}, s32[4,1326]{1,0:T(4,128)}, u32[]{:S(2)}) copy-start(s32[4,1326]{1,0:T(4,128)} %rank_hbm.1) | copy-start | bytes 63652
  6.4 0.7 %copy-start.6 = (s32[2,1408]{1,0:T(2,128)S(1)}, s32[2,1408]{1,0:T(2,128)}, u32[]{:S(2)}) copy-start(s32[2,1408]{1,0:T(2,128)} %constant.4.clone.bits_hbm) | copy-start | bytes 33796

commit v2 on v1

--- a/solution.py
+++ b/solution.py
@@ -16,6 +16,7 @@
 COLUMNS = 16
 BOARD_DEV = 4
 ROWS = 24
+BLOCK = 64
 HALF = 16
 MESH = pl.DeviceIdType.MESH
 
@@ -48,14 +49,15 @@
 
 
 def slot(ref, index, rows):
-    return ref.at[pl.ds(pl.multiple_of(index * rows, 8), rows), :]
+    used = 2 * TILES if rows == ROWS else TILES
+    return ref.at[pl.ds(pl.multiple_of(index * rows, 8), used), :]
 
 
 def kernel(
     root_hbm, front_hbm, stop_hbm, go_hbm, live_hbm, cards_hbm, rank_hbm, bits_hbm, scan_hbm,
     out_stop, out_go, out_sec,
     root_v, front_v, stop_v, go_v, live_s, cards_s, rank_v, bits_v, scan_v,
-    pad, asend, arecv, ends, colrow, cols, bcast, w, lsc, lhs, leafsc,
+    pad, asend, arecv, ends, bitrow, rankrow, bitwide, rankwide, bitcol, rankcol, w, lsc, lhs, leafsc,
     gsend, grecv, nsc, rsend, rrecv, fsend, frecv,
     in_sem, a_ss, a_rs, g_ss, g_rs, r_ss, r_rs, f_ss, f_rs,
 ):
@@ -158,29 +160,40 @@
         at = pl.multiple_of((index * NODES + node) * ROWS, 8)
         return jnp.where(mask > 0, ends[pl.ds(at, ROWS), :], 0.0)
 
-    colrow[...] = jnp.zeros(colrow.shape, jnp.int32)
-    colrow[0:2, :] = bits_v[...]
+    bitrow[...] = jnp.zeros(bitrow.shape, jnp.int32)
+    bitrow[0:2, :] = bits_v[...]
+    rankrow[...] = jnp.zeros(rankrow.shape, jnp.float32)
     for jj in range(2):
-        colrow[2 + jj : 3 + jj, :H] = rank_v[pl.ds(2 * core + jj, 1), :]
-    for r in range(4):
-        bcast[r] = jnp.broadcast_to(colrow[r : r + 1, :], (8, HP))
+        rankrow[jj : jj + 1, :H] = rank_v[pl.ds(2 * core + jj, 1), :].astype(jnp.float32)
+    for r in range(2):
+        bitwide[r] = jnp.broadcast_to(bitrow[r : r + 1, :], (8, HP))
+        rankwide[r] = jnp.broadcast_to(rankrow[r : r + 1, :], (8, HP))
     for t in range(TILES):
-        cols[128 * t : 128 * (t + 1), :] = colrow[:, 128 * t : 128 * (t + 1)].T
+        lanes = slice(128 * t, 128 * (t + 1))
+        bitcol[lanes, :] = bitrow[:, lanes].T
+        rankcol[lanes, :] = rankrow[:, lanes].T
 
     def payoff_rows(block, _):
-        at = pl.multiple_of(block * 16, 16)
-        col_of = cols[pl.ds(at, 16), :]
-        wide = [jnp.broadcast_to(col_of[:, r : r + 1], (16, 128)) for r in range(4)]
+        at = [pl.multiple_of(block * BLOCK + 16 * i, 16) for i in range(BLOCK // 16)]
+        wide = [
+            [jnp.broadcast_to(ref[pl.ds(a, 16), r : r + 1], (16, 128)) for ref in (bitcol, rankcol) for r in range(2)]
+            for a in at
+        ]
+        one = jnp.bfloat16(1)
         for t in range(TILES):
             lanes = slice(128 * t, 128 * (t + 1))
-            row = [jnp.concatenate([bcast[r, :, lanes]] * 2, axis=0) for r in range(4)]
-            free = ((wide[0] & row[0]) | (wide[1] & row[1])) == 0
-            for jj in range(2):
-                step = jnp.minimum(jnp.maximum(row[2 + jj] - wide[2 + jj], -1), 1)
-                w[jj, pl.ds(at, 16), lanes] = jnp.where(free, step, 0).astype(jnp.float32).astype(jnp.bfloat16)
+            low, high, rank0, rank1 = (
+                jnp.concatenate([ref[r, :, lanes]] * 2, axis=0) for ref in (bitwide, rankwide) for r in range(2)
+            )
+            for a, (low_g, high_g, rank0_g, rank1_g) in zip(at, wide):
+                shared = (low_g & low) | (high_g & high)
+                free = jnp.where(shared == 0, 1.0, 0.0).astype(jnp.bfloat16)
+                for jj, step in enumerate((rank0 - rank0_g, rank1 - rank1_g)):
+                    step = step.astype(jnp.bfloat16)
+                    w[jj, pl.ds(a, 16), lanes] = jnp.minimum(jnp.maximum(step, -one), one) * free
         return 0
 
-    lax.fori_loop(0, HP // 16, payoff_rows, 0)
+    lax.fori_loop(0, HP // BLOCK, payoff_rows, 0)
 
     for d in range(1, SECTIONS):
         other = (me + d) % SECTIONS
@@ -227,7 +240,7 @@
         to = 2 * node + to_core
         s = (to_col + to) % SECTIONS
         return remote(
-            slot(rsend, 2 * s + to_core, HALF), rrecv.at[dc * COLUMNS + db], r_ss.at[dc * COLUMNS + db],
+            slot(rsend, 2 * s + to_core, HALF), slot(rrecv, dc * COLUMNS + db, HALF), r_ss.at[dc * COLUMNS + db],
             r_rs.at[dc * COLUMNS + db], to, to_col,
         )
 
@@ -248,11 +261,12 @@
     total = rsend[pl.ds(pl.multiple_of((2 * mine + core) * HALF, 8), HALF), :]
     for dc, db in pairs:
         r_copy(dc, db).wait_recv()
-        total = total + rrecv[dc * COLUMNS + db]
+        at = (dc * COLUMNS + db) * HALF
+        total = total + rrecv[at : at + HALF, :]
     fsend[...] = total / total[TILES - 1 : TILES, 127:128]
 
     def f_copy(db):
-        return remote(fsend, slot(frecv, me, HALF), f_ss.at[db], f_rs.at[me], mine, (col + db) % COLUMNS)
+        return remote(slot(fsend, 0, HALF), slot(frecv, me, HALF), f_ss.at[db], f_rs.at[me], mine, (col + db) % COLUMNS)
 
     for db in range(1, COLUMNS):
         f_copy(db).start()
@@ -283,7 +297,7 @@
     for k in range(SECTIONS):
         @pl.when(jnp.logical_or(me != k, col != 0))
         def _(k=k):
-            remote(fsend, slot(frecv, k, HALF), f_ss.at[0], f_rs.at[k], mine, col).wait_recv()
+            remote(slot(fsend, 0, HALF), slot(frecv, k, HALF), f_ss.at[0], f_rs.at[k], mine, col).wait_recv()
     for p in range(2):
         for t in range(TILES):
             size = 128 if t < TILES - 1 else LAST
@@ -327,19 +341,20 @@
             pltpu.VMEM((BOARD_DEV, NODES, 128), f32),
             pltpu.VMEM((SECTIONS * ROWS, 128), f32), pltpu.VMEM((SECTIONS * ROWS, 128), f32),
             pltpu.VMEM((4 * NODES * ROWS, 128), f32),
-            pltpu.VMEM((8, HP), i32), pltpu.VMEM((HP, 8), i32), pltpu.VMEM((4, 8, HP), i32),
+            pltpu.VMEM((8, HP), i32), pltpu.VMEM((8, HP), f32), pltpu.VMEM((2, 8, HP), i32), pltpu.VMEM((2, 8, HP), f32),
+            pltpu.VMEM((HP, 8), i32), pltpu.VMEM((HP, 8), f32),
             pltpu.VMEM((2, HP, HP), jnp.bfloat16),
             pltpu.VMEM((2, SECTIONS * ROWS, 128), f32), pltpu.VMEM((2, 2 * SECTIONS, HP), jnp.bfloat16),
             pltpu.VMEM((2, SECTIONS * ROWS, 128), f32),
             pltpu.VMEM((SECTIONS * ROWS, 128), f32), pltpu.VMEM((SECTIONS * ROWS, 128), f32),
             pltpu.VMEM((2 * SECTIONS * ROWS, 128), f32),
-            pltpu.VMEM((2 * SECTIONS * HALF, 128), f32), pltpu.VMEM((2 * COLUMNS, HALF, 128), f32),
+            pltpu.VMEM((2 * SECTIONS * HALF, 128), f32), pltpu.VMEM((2 * COLUMNS * HALF, 128), f32),
             pltpu.VMEM((HALF, 128), f32), pltpu.VMEM((SECTIONS * HALF, 128), f32),
             dma((9,)), dma((SECTIONS,)), dma((SECTIONS,)), dma((SECTIONS,)), dma((SECTIONS,)),
             dma((2 * COLUMNS,)), dma((2 * COLUMNS,)), dma((COLUMNS,)), dma((SECTIONS,)),
         ],
         compiler_params=pltpu.CompilerParams(
-            collective_id=0, has_side_effects=True, vmem_limit_bytes=40 * 1024 * 1024
+            collective_id=0, has_side_effects=True, vmem_limit_bytes=67043328
         ),
     )(
         root_reach, frontier_value, regret_stop[0], regret_go[0], board_live, board_cards, hand_rank,

time: 52.6 us -> 39 us (0.74)
  Pallas kernels: 42.9 us -> 34.6 us
  local copies, waits for them, and re-layouts: 8.45 us -> 3.22 us
    pallas_call x1, Pallas kernels: 42.9 us -> 34.6 us  [local(): pl.pallas_call(kernel, out_shape=(jax.ShapeDtypeStruct(regrets, f32), jax...]
    unnamed x21 -> x7, local copies, waits for them, and re-layouts: 8.45 us -> 3.22 us
where the time goes in v2:
time: 39 us; the launch traced here: 38.4 us
  Pallas kernels  34.6 us (89%)
  local copies, waits for them, and re-layouts  3.22 us (8%)
  between operations  0.65 us (2%)
    pallas_call x1, Pallas kernels, local(): pl.pallas_call(kernel, out_shape=(jax.ShapeDtypeStruct(regrets, f32), jax...  34.6 us
    unnamed x7, local copies, waits for them, and re-layouts  3.22 us

profile of v2, /device:TPU:1, one launch (start us, length us, event | category | flops | bytes accessed | tf_op | source)
XLA Modules:
  0.0 38.4 jit_solution(16671589991045945402)
XLA Ops:
  0.6 34.6 %shard_map.112 = (f32[4,8,1326]{2,1,0:T(8,128)}, f32[4,8,1326]{2,1,0:T(8,128)}, f32[2,8,1326]{2,1,0:T(8,128)}) custom-call(f32[2,8,1326]{2,1,0:T(8,128)} %root_hbm.1, f32[2,8,1326]{2,1,0:T(8,128)} %front_hbm.1, f32[4,8,1326]{2,1,0:T(8,128)} %bitcast.7, f32[4,8,1326]{2,1,0:T(8,128)} %bitcast.8, s32[4]{0:T(128)} %live_hbm.1, s32[4,5]{1,0:T(4,128)} %cards_hbm.1, ...), custom_call_target="tpu_custom_call" | custom-call | tf_op jit(solution)/shard_map/pallas_call | solution.py:328
  35.2 0.0 copy-start
  35.2 1.6 %copy.15 = f32[1,4,8,1326]{3,2,1,0:T(8,128)} copy(f32[1,4,8,1326]{3,2,1,0:T(8,128)} %bitcast.6) | data formatting | bytes 339456
  36.9 0.0 copy-done
  36.9 0.0 copy-start.1
  36.9 0.7 %copy.16 = f32[1,4,8,1326]{3,2,1,0:T(8,128)} copy(f32[1,4,8,1326]{3,2,1,0:T(8,128)S(1)} %bitcast.5) | data formatting | bytes 339456
  37.5 0.3 copy-done.1
  37.8 0.6 %copy.17 = f32[1,2,8,1326]{3,2,1,0:T(8,128)} copy(f32[1,2,8,1326]{3,2,1,0:T(8,128)S(1)} %bitcast.9) | data formatting | bytes 169728
Async XLA Ops:
  35.2 1.7 %copy-start = (f32[4,8,1326]{2,1,0:T(8,128)S(1)}, f32[4,8,1326]{2,1,0:T(8,128)}, u32[]{:S(2)}) copy-start(f32[4,8,1326]{2,1,0:T(8,128)} %get-tuple-element.7) | copy-start | bytes 509188
  36.9 0.9 %copy-start.1 = (f32[2,8,1326]{2,1,0:T(8,128)S(1)}, f32[2,8,1326]{2,1,0:T(8,128)}, u32[]{:S(2)}) copy-start(f32[2,8,1326]{2,1,0:T(8,128)} %get-tuple-element.8) | copy-start | bytes 254596

commit v3 on v2

--- a/solution.py
+++ b/solution.py
@@ -19,6 +19,7 @@
 BLOCK = 64
 HALF = 16
 MESH = pl.DeviceIdType.MESH
+FAR = sorted(range(COLUMNS), key=lambda d: -min(d // 4, 4 - d // 4) - min(d % 4, 4 - d % 4))
 
 
 def hand_bits():
@@ -53,19 +54,42 @@
     return ref.at[pl.ds(pl.multiple_of(index * rows, 8), used), :]
 
 
+def wait_rows(ref, rows, sem):
+    some = ref.at[pl.ds(0, rows), :]
+    pltpu.make_async_copy(some, some, sem).wait()
+
+
 def kernel(
     root_hbm, front_hbm, stop_hbm, go_hbm, live_hbm, cards_hbm, rank_hbm, bits_hbm, scan_hbm,
     out_stop, out_go, out_sec,
-    root_v, front_v, stop_v, go_v, live_s, cards_s, rank_v, bits_v, scan_v,
+    root_v, front_v, regret_v, live_s, cards_s, rank_v, bits_v, scan_v,
     pad, asend, arecv, ends, bitrow, rankrow, bitwide, rankwide, bitcol, rankcol, w, lsc, lhs, leafsc,
     gsend, grecv, nsc, rsend, rrecv, fsend, frecv,
-    in_sem, a_ss, a_rs, g_ss, g_rs, r_ss, r_rs, f_ss, f_rs,
+    in_sem, regret_sem, a_ss, a_rs, g_ss, g_rs, r_ss, r_rs, f_ss, f_rs,
 ):
     me = lax.axis_index("section")
     col = lax.axis_index("board")
     node = me // 2
     core = me % 2
-
+    row, lane = col // 4, col % 4
+
+    def column(db):
+        return (row + db // 4) % 4 * 4 + (lane + db % 4) % 4
+
+    loads = [
+        pltpu.make_async_copy(src, dst, in_sem.at[i])
+        for i, (src, dst) in enumerate(
+            [
+                (root_hbm, root_v), (front_hbm, front_v),
+                (live_hbm, live_s), (cards_hbm, cards_s), (rank_hbm, rank_v), (bits_hbm, bits_v),
+                (scan_hbm, scan_v),
+            ]
+        )
+    ]
+    for i, src in enumerate((stop_hbm, go_hbm)):
+        pltpu.make_async_copy(src, regret_v.at[i], regret_sem).start()
+    for copy in loads:
+        copy.start()
     barrier = pltpu.get_barrier_semaphore()
     for d in range(1, SECTIONS):
         pl.semaphore_signal(
@@ -76,43 +100,30 @@
             pl.semaphore_signal(
                 barrier,
                 inc=1,
-                device_id={"section": 2 * node + (core + dc) % 2, "board": (col + db) % COLUMNS},
+                device_id={"section": 2 * node + (core + dc) % 2, "board": column(db)},
                 device_id_type=MESH,
             )
 
-    loads = [
-        pltpu.make_async_copy(src, dst, in_sem.at[i])
-        for i, (src, dst) in enumerate(
-            [
-                (stop_hbm, stop_v), (go_hbm, go_v), (root_hbm, root_v), (front_hbm, front_v),
-                (live_hbm, live_s), (cards_hbm, cards_s), (rank_hbm, rank_v), (bits_hbm, bits_v),
-                (scan_hbm, scan_v),
-            ]
-        )
-    ]
-    for copy in loads:
-        copy.start()
     pad[...] = jnp.full(pad.shape, 0.5, jnp.float32)
     ends[...] = jnp.zeros(ends.shape, jnp.float32)
-    loads[0].wait()
-    loads[1].wait()
+    pltpu.make_async_copy(regret_v, regret_v, regret_sem).wait()
 
     for j in range(BOARD_DEV):
         for t in range(TILES):
             if t < TILES - 1:
                 at = pl.ds(128 * t, 128)
-                tile = go_v[j, :, at] / (go_v[j, :, at] + stop_v[j, :, at])
+                tile = regret_v[1, j, :, at] / (regret_v[1, j, :, at] + regret_v[0, j, :, at])
             else:
                 at = pl.ds(128 * t, LAST)
-                pad[j, :, :LAST] = go_v[j, :, at] / (go_v[j, :, at] + stop_v[j, :, at])
+                pad[j, :, :LAST] = regret_v[1, j, :, at] / (regret_v[1, j, :, at] + regret_v[0, j, :, at])
                 tile = pad[j]
-            row = (j // 2) * ROWS + (j % 2) * TILES + t
-            asend[pl.ds(row, NODES, stride=2 * ROWS), :] = tile
+            at_row = (j // 2) * ROWS + (j % 2) * TILES + t
+            asend[pl.ds(at_row, NODES, stride=2 * ROWS), :] = tile
     pl.semaphore_wait(barrier, SECTIONS - 1 + 2 * (COLUMNS - 1))
 
     def a_copy(to):
         return remote(
-            slot(asend, to, ROWS), slot(arecv, me, ROWS), a_ss.at[to], a_rs.at[me], to, col
+            slot(asend, to, ROWS), slot(arecv, me, ROWS), a_ss, a_rs, to, col
         )
 
     order = sorted(range(1, SECTIONS), key=lambda d: -min(d, SECTIONS - d))
@@ -121,7 +132,7 @@
     own = pl.ds(pl.multiple_of(me * ROWS, 8), ROWS)
     arecv[own, :] = asend[own, :]
 
-    for copy in loads[2:]:
+    for copy in loads:
         copy.wait()
 
     alive = []
@@ -195,9 +206,7 @@
 
     lax.fori_loop(0, HP // BLOCK, payoff_rows, 0)
 
-    for d in range(1, SECTIONS):
-        other = (me + d) % SECTIONS
-        remote(slot(asend, other, ROWS), slot(arecv, other, ROWS), a_ss.at[other], a_rs.at[other], other, col).wait_recv()
+    wait_rows(arecv, (SECTIONS - 1) * 2 * TILES, a_rs)
 
     reach = [end_of(0), end_of(1)]
     for s in range(SECTIONS):
@@ -236,21 +245,20 @@
 
     def r_copy(dc, db):
         to_core = (core + dc) % 2
-        to_col = (col + db) % COLUMNS
+        to_col = column(db)
         to = 2 * node + to_core
         s = (to_col + to) % SECTIONS
         return remote(
-            slot(rsend, 2 * s + to_core, HALF), slot(rrecv, dc * COLUMNS + db, HALF), r_ss.at[dc * COLUMNS + db],
-            r_rs.at[dc * COLUMNS + db], to, to_col,
+            slot(rsend, 2 * s + to_core, HALF), slot(rrecv, dc * COLUMNS + db, HALF), r_ss, r_rs, to, to_col,
         )
 
-    pairs = [(dc, db) for db in range(COLUMNS) for dc in range(2) if dc or db]
+    pairs = [(dc, db) for db in FAR for dc in range(2) if dc or db]
     for dc, db in pairs:
         r_copy(dc, db).start()
 
     def g_copy(to):
         return remote(
-            slot(gsend, to, ROWS), slot(grecv, me, ROWS), g_ss.at[to], g_rs.at[me], to, col
+            slot(gsend, to, ROWS), slot(grecv, me, ROWS), g_ss, g_rs, to, col
         )
 
     for d in order:
@@ -259,16 +267,16 @@
 
     mine = (col + me) % SECTIONS
     total = rsend[pl.ds(pl.multiple_of((2 * mine + core) * HALF, 8), HALF), :]
+    wait_rows(rrecv, (2 * COLUMNS - 1) * TILES, r_rs)
     for dc, db in pairs:
-        r_copy(dc, db).wait_recv()
         at = (dc * COLUMNS + db) * HALF
         total = total + rrecv[at : at + HALF, :]
     fsend[...] = total / total[TILES - 1 : TILES, 127:128]
 
     def f_copy(db):
-        return remote(slot(fsend, 0, HALF), slot(frecv, me, HALF), f_ss.at[db], f_rs.at[me], mine, (col + db) % COLUMNS)
-
-    for db in range(1, COLUMNS):
+        return remote(slot(fsend, 0, HALF), slot(frecv, me, HALF), f_ss, f_rs, mine, column(db))
+
+    for db in FAR[:-1]:
         f_copy(db).start()
 
     @pl.when(col != 0)
@@ -279,42 +287,53 @@
     def _():
         frecv[pl.ds(pl.multiple_of(me * HALF, 8), HALF), :] = fsend[...]
 
-    for d in range(1, SECTIONS):
-        other = (me + d) % SECTIONS
-        remote(slot(gsend, other, ROWS), slot(grecv, other, ROWS), g_ss.at[other], g_rs.at[other], other, col).wait_recv()
+    wait_rows(grecv, (SECTIONS - 1) * 2 * TILES, g_rs)
     for j in range(BOARD_DEV):
         keep = live_s[j] > 0
         for t in range(TILES):
             size = 128 if t < TILES - 1 else LAST
             at = pl.ds(128 * t, size)
             gap = grecv[pl.ds((j // 2) * ROWS + (j % 2) * TILES + t, NODES, stride=2 * ROWS), :][:, :size]
-            stop = stop_v[j, :, at]
-            go = go_v[j, :, at]
+            stop = regret_v[0, j, :, at]
+            go = regret_v[1, j, :, at]
             total_regret = stop + go
             out_stop[j, :, at] = jnp.where(keep, jnp.maximum(stop + go / total_regret * gap, 0.0), stop)
             out_go[j, :, at] = jnp.where(keep, jnp.maximum(go - stop / total_regret * gap, 0.0), go)
 
-    for k in range(SECTIONS):
-        @pl.when(jnp.logical_or(me != k, col != 0))
-        def _(k=k):
-            remote(slot(fsend, 0, HALF), slot(frecv, k, HALF), f_ss.at[0], f_rs.at[k], mine, col).wait_recv()
+    wait_rows(asend, (SECTIONS - 1) * 2 * TILES, a_ss)
+    wait_rows(gsend, (SECTIONS - 1) * 2 * TILES, g_ss)
+    wait_rows(rsend, (2 * COLUMNS - 1) * TILES, r_ss)
+
+    @pl.when(col != 0)
+    def _():
+        wait_rows(frecv, COLUMNS * TILES, f_ss)
+
+    @pl.when(col == 0)
+    def _():
+        wait_rows(frecv, (COLUMNS - 1) * TILES, f_ss)
+
+    @pl.when(col != 0)
+    def _():
+        wait_rows(frecv, SECTIONS * TILES, f_rs)
+
+    @pl.when(col == 0)
+    def _():
+        wait_rows(frecv, (SECTIONS - 1) * TILES, f_rs)
+
     for p in range(2):
         for t in range(TILES):
             size = 128 if t < TILES - 1 else LAST
             tile = frecv[pl.ds(p * HALF + t, NODES, stride=2 * HALF), :]
             out_sec[p, :, pl.ds(128 * t, size)] = tile[:, :size]
 
-    for d in order:
-        a_copy((me + d) % SECTIONS).wait_send()
-        g_copy((me + d) % SECTIONS).wait_send()
-    for dc, db in pairs:
-        r_copy(dc, db).wait_send()
-    for db in range(1, COLUMNS):
-        f_copy(db).wait_send()
-
-    @pl.when(col != 0)
-    def _():
-        f_copy(0).wait_send()
+
+def store(stop_v, go_v, sec_v, out_stop, out_go, out_sec, sem):
+    pairs = ((stop_v, out_stop), (go_v, out_go), (sec_v, out_sec))
+    copies = [pltpu.make_async_copy(src, dst.at[0], sem.at[i]) for i, (src, dst) in enumerate(pairs)]
+    for copy in copies:
+        copy.start()
+    for copy in copies:
+        copy.wait()
 
 
 def local(root_reach, frontier_value, regret_stop, regret_go, board_live, board_cards, hand_rank):
@@ -322,20 +341,24 @@
     f32, i32 = jnp.float32, jnp.int32
     regrets = (BOARD_DEV, NODES, H)
     ends = (2, NODES, H)
-    any_spec = pl.BlockSpec(memory_space=pl.ANY)
+    hbm_spec = pl.BlockSpec(memory_space=pltpu.HBM)
     vmem_spec = pl.BlockSpec(memory_space=pltpu.VMEM)
     dma = pltpu.SemaphoreType.DMA
+    operands = (
+        root_reach, frontier_value, regret_stop[0], regret_go[0], board_live, board_cards, hand_rank,
+        jnp.asarray(bits), jnp.asarray(scan),
+    )
     new_stop, new_go, section_value = pl.pallas_call(
         kernel,
         out_shape=(
-            jax.ShapeDtypeStruct(regrets, f32),
-            jax.ShapeDtypeStruct(regrets, f32),
-            jax.ShapeDtypeStruct(ends, f32),
+            pltpu.VMEM(regrets, f32),
+            pltpu.VMEM(regrets, f32),
+            pltpu.VMEM(ends, f32),
         ),
-        in_specs=[any_spec] * 9,
+        in_specs=[hbm_spec] * 9,
         out_specs=(vmem_spec,) * 3,
         scratch_shapes=[
-            pltpu.VMEM(ends, f32), pltpu.VMEM(ends, f32), pltpu.VMEM(regrets, f32), pltpu.VMEM(regrets, f32),
+            pltpu.VMEM(ends, f32), pltpu.VMEM(ends, f32), pltpu.VMEM((2, *regrets), f32),
             pltpu.SMEM((BOARD_DEV,), i32), pltpu.SMEM((BOARD_DEV, 5), i32), pltpu.VMEM((BOARD_DEV, H), i32),
             pltpu.VMEM((2, HP), i32), pltpu.VMEM((2 * ROWS, 128), i32),
             pltpu.VMEM((BOARD_DEV, NODES, 128), f32),
@@ -350,17 +373,24 @@
             pltpu.VMEM((2 * SECTIONS * ROWS, 128), f32),
             pltpu.VMEM((2 * SECTIONS * HALF, 128), f32), pltpu.VMEM((2 * COLUMNS * HALF, 128), f32),
             pltpu.VMEM((HALF, 128), f32), pltpu.VMEM((SECTIONS * HALF, 128), f32),
-            dma((9,)), dma((SECTIONS,)), dma((SECTIONS,)), dma((SECTIONS,)), dma((SECTIONS,)),
-            dma((2 * COLUMNS,)), dma((2 * COLUMNS,)), dma((COLUMNS,)), dma((SECTIONS,)),
+            dma((7,)), *([dma] * 9),
         ],
         compiler_params=pltpu.CompilerParams(
-            collective_id=0, has_side_effects=True, vmem_limit_bytes=67043328
+            collective_id=0, has_side_effects=True, vmem_limit_bytes=32 * 1024 * 1024
         ),
-    )(
-        root_reach, frontier_value, regret_stop[0], regret_go[0], board_live, board_cards, hand_rank,
-        jnp.asarray(bits), jnp.asarray(scan),
-    )
-    return new_stop[None], new_go[None], section_value[None]
+    )(*(pltpu.with_memory_space_constraint(x, pltpu.HBM) for x in operands))
+    return pl.pallas_call(
+        store,
+        out_shape=(
+            jax.ShapeDtypeStruct((1, *regrets), f32),
+            jax.ShapeDtypeStruct((1, *regrets), f32),
+            jax.ShapeDtypeStruct((1, *ends), f32),
+        ),
+        in_specs=[vmem_spec] * 3,
+        out_specs=(hbm_spec,) * 3,
+        scratch_shapes=[dma((3,))],
+        compiler_params=pltpu.CompilerParams(vmem_limit_bytes=1024 * 1024),
+    )(new_stop, new_go, section_value)
 
 
 def solution(mesh):

time: 39 us -> 33.6 us (0.86); the launches traced: 38.4 us -> 33.5 us
  local copies, waits for them, and re-layouts: 3.22 us -> 0 us
  Pallas kernels: 34.6 us -> 32.8 us
    unnamed x7 -> x0, local copies, waits for them, and re-layouts: 3.22 us -> none
    pallas_call x1 -> x2, Pallas kernels: 34.6 us -> 32.8 us  [the longest x1 32.1 us: local(): pl.pallas_call(kernel, out_shape=(pltpu.VMEM(regrets, f32), pltpu.VMEM(re...]
where the time goes in v3:
time: 33.6 us; the launch traced here: 33.5 us
  Pallas kernels  32.8 us (98%)
  between operations  0.64 us (2%)
    pallas_call x1, Pallas kernels, local(): pl.pallas_call(kernel, out_shape=(pltpu.VMEM(regrets, f32), pltpu.VMEM(re...  32.1 us
    pallas_call x1, Pallas kernels, local(): pl.pallas_call(store, out_shape=(jax.ShapeDtypeStruct((1, *regrets), f32)...  0.79 us

profile of v3, /device:TPU:1, one launch (start us, length us, event | category | flops | bytes accessed | tf_op | source)
XLA Modules:
  0.0 33.5 jit_solution(14551966397968348079)
XLA Ops:
  0.6 32.1 %shard_map.112 = (f32[4,8,1326]{2,1,0:T(8,128)S(1)}, f32[4,8,1326]{2,1,0:T(8,128)S(1)}, f32[2,8,1326]{2,1,0:T(8,128)S(1)}) custom-call(f32[2,8,1326]{2,1,0:T(8,128)} %root_hbm.1, f32[2,8,1326]{2,1,0:T(8,128)} %front_hbm.1, f32[4,8,1326]{2,1,0:T(8,128)} %bitcast.2, f32[4,8,1326]{2,1,0:T(8,128)} %bitcast.3, s32[4]{0:T(128)} %live_hbm.1, s32[4,5]{1,0:T(4,128)} %cards_hbm.1, ...), custom_call_target="tpu_custom_call" | custom-call | tf_op jit(solution)/shard_map/pallas_call | solution.py:351
  32.7 0.8 %shard_map.113 = (f32[1,4,8,1326]{3,2,1,0:T(8,128)}, f32[1,4,8,1326]{3,2,1,0:T(8,128)}, f32[1,2,8,1326]{3,2,1,0:T(8,128)}) custom-call(f32[4,8,1326]{2,1,0:T(8,128)S(1)} %get-tuple-element.6.stop_v, f32[4,8,1326]{2,1,0:T(8,128)S(1)} %get-tuple-element.7.go_v, f32[2,8,1326]{2,1,0:T(8,128)S(1)} %get-tuple-element.8.sec_v), custom_call_target="tpu_custom_call" | custom-call | tf_op jit(solution)/shard_map/pallas_call | solution.py:382

commit v4 on v3

v4 whole, which is shorter than its diff:
```python
import jax
import jax.numpy as jnp
import numpy as np
from jax import lax
from jax.experimental import pallas as pl
from jax.experimental.pallas import tpu as pltpu
from jax.sharding import PartitionSpec as P

CARDS = 52
H = 1326
NODES = 8
TILES = 11
HP = TILES * 128
LAST = H - 128 * (TILES - 1)
SECTIONS = 16
COLUMNS = 16
BOARD_DEV = 4
UNIT = 24
BLOCK = 32
HALF = 16
MESH = pl.DeviceIdType.MESH
ORDER = sorted(range(1, SECTIONS), key=lambda d: -min(d, SECTIONS - d))
FAR = sorted(range(COLUMNS), key=lambda d: -min(d // 4, 4 - d // 4) - min(d % 4, 4 - d % 4))


def hand_bits():
    first, second = np.triu_indices(CARDS, 1)
    low = np.full((HP,), -1, np.int64)
    high = np.full((HP,), -1, np.int64)
    both = (np.int64(1) << first) | (np.int64(1) << second)
    low[:H] = both & 0xFFFFFFFF
    high[:H] = both >> 32
    rows = np.stack([low, high]).astype(np.uint32).view(np.int32)
    return rows, rows.reshape(2, TILES, 128)


def remote(src, dst, send, recv, section, board):
    return pltpu.make_async_remote_copy(
        src_ref=src,
        dst_ref=dst,
        send_sem=send,
        recv_sem=recv,
        device_id={"section": section, "board": board},
        device_id_type=MESH,
    )


def unit(ref, index, stride=UNIT):
    return ref.at[pl.ds(pl.multiple_of(index * stride, 8), TILES), :]


def wait_rows(ref, rows, sem):
    some = ref.at[pl.ds(0, rows), :]
    pltpu.make_async_copy(some, some, sem).wait()


def kernel(
    root_hbm, front_hbm, stop_hbm, go_hbm, live_hbm, cards_hbm, rank_hbm, bits_hbm, scan_hbm,
    out_stop, out_go, out_sec,
    root_v, front_v, regret_v, live_s, cards_s, rank_v, bits_v, scan_v,
    pad, asend, arecv, ends, bitrow, rankrow, bitwide, rankwide, bitcol, rankcol, w, lsc, lhs, leafsc,
    gsend, grecv, rsend, rrecv, fsend, frecv,
    in_sem, regret_sem, a_ss, a_rs, g_ss, g_rs, r_ss, r_rs, f_ss, f_rs,
):
    me = lax.axis_index("section")
    col = lax.axis_index("board")
    node = me // 2
    core = me % 2
    row, lane = col // 4, col % 4

    def column(db):
        return (row + db // 4) % 4 * 4 + (lane + db % 4) % 4

    loads = [
        pltpu.make_async_copy(src, dst, in_sem.at[i])
        for i, (src, dst) in enumerate(
            [
                (root_hbm, root_v), (front_hbm, front_v),
                (live_hbm, live_s), (cards_hbm, cards_s), (rank_hbm, rank_v), (bits_hbm, bits_v),
                (scan_hbm, scan_v),
            ]
        )
    ]
    for i, src in enumerate((stop_hbm, go_hbm)):
        pltpu.make_async_copy(src, regret_v.at[i], regret_sem).start()
    for copy in loads:
        copy.start()
    barrier = pltpu.get_barrier_semaphore()

    def greet(section, board):
        pl.semaphore_signal(barrier, inc=1, device_id={"section": section, "board": board}, device_id_type=MESH)

    for d in ORDER:
        greet((me + d) % SECTIONS, col)
    for db in FAR[:-1]:
        for dc in range(2):
            greet(2 * node + (core + dc) % 2, column(db))
    pad[...] = jnp.full(pad.shape, 0.5, jnp.float32)
    ends[...] = jnp.zeros(ends.shape, jnp.float32)
    pltpu.make_async_copy(regret_v, regret_v, regret_sem).wait()

    for j in range(BOARD_DEV):
        for t in range(TILES):
            if t < TILES - 1:
                at = pl.ds(128 * t, 128)
                tile = regret_v[1, j, :, at] / (regret_v[1, j, :, at] + regret_v[0, j, :, at])
            else:
                at = pl.ds(128 * t, LAST)
                pad[j, :, :LAST] = regret_v[1, j, :, at] / (regret_v[1, j, :, at] + regret_v[0, j, :, at])
                tile = pad[j]
            first = (j % 2 * 2 + j // 2) * NODES * UNIT
            asend[pl.ds(first + t, NODES, stride=UNIT), :] = tile
    for copy in loads:
        copy.wait()

    alive = []
    board_bits = []
    for jj in range(2):
        j = 2 * core + jj
        alive.append(jnp.where(live_s[j] > 0, 1.0, 0.0).astype(jnp.float32))
        low = jnp.int32(0)
        high = jnp.int32(0)
        for i in range(5):
            card = cards_s[j, i]
            bit = lax.shift_left(jnp.int32(1), card % 32)
            low = low | jnp.where(card < 32, bit, 0)
            high = high | jnp.where(card < 32, 0, bit)
        board_bits.append((low, high))
    inside = (scan_v[0] & scan_v[1]) != -1
    mask = [
        jnp.where(((scan_v[0] & low) | (scan_v[1] & high)) == 0, 1.0, 0.0).astype(jnp.float32)
        for low, high in board_bits
    ]

    for which, ref in enumerate((root_v, front_v)):
        for p in range(2):
            base = (2 * which + p) * NODES * UNIT
            pad[p, :, :] = jnp.zeros((NODES, 128), jnp.float32)
            pad[p, :, :LAST] = ref[p, :, pl.ds(128 * (TILES - 1), LAST)]
            for t in range(TILES):
                tile = ref[p, :, pl.ds(128 * t, 128)] if t < TILES - 1 else pad[p]
                ends[pl.ds(base + t, NODES, stride=UNIT), :] = tile

    def end_of(index, jj):
        return unit(ends, index * NODES + node)[...] * mask[jj]

    bitrow[...] = jnp.zeros(bitrow.shape, jnp.int32)
    bitrow[0:2, :] = bits_v[...]
    rankrow[...] = jnp.zeros(rankrow.shape, jnp.float32)
    for jj in range(2):
        rankrow[jj : jj + 1, :H] = rank_v[pl.ds(2 * core + jj, 1), :].astype(jnp.float32)
    for r in range(2):
        bitwide[r] = jnp.broadcast_to(bitrow[r : r + 1, :], (8, HP))
        rankwide[r] = jnp.broadcast_to(rankrow[r : r + 1, :], (8, HP))
    for t in range(TILES):
        lanes = slice(128 * t, 128 * (t + 1))
        bitcol[lanes, :] = bitrow[:, lanes].T
        rankcol[lanes, :] = rankrow[:, lanes].T

    pl.semaphore_wait(barrier, SECTIONS - 1 + 2 * (COLUMNS - 1))

    def a_unit(jj, to):
        return (2 * jj + to % 2) * NODES + to // 2

    def a_copy(jj, to):
        return remote(
            unit(asend, a_unit(jj, to)), unit(arecv, jj * SECTIONS + me), a_ss, a_rs.at[jj], to, col
        )

    for jj in range(2):
        for d in ORDER:
            a_copy(jj, (me + d) % SECTIONS).start()
    for jj in range(2):
        unit(arecv, jj * SECTIONS + me)[...] = unit(asend, a_unit(jj, me))[...]

    def payoff_rows(block, _):
        at = [pl.multiple_of(block * BLOCK + 16 * i, 16) for i in range(BLOCK // 16)]
        wide = [
            [jnp.broadcast_to(ref[pl.ds(a, 16), r : r + 1], (16, 128)) for ref in (bitcol, rankcol) for r in range(2)]
            for a in at
        ]
        one = jnp.bfloat16(1)
        for t in range(TILES):
            lanes = slice(128 * t, 128 * (t + 1))
            low, high, rank0, rank1 = (
                jnp.concatenate([ref[r, :, lanes]] * 2, axis=0) for ref in (bitwide, rankwide) for r in range(2)
            )
            for a, (low_g, high_g, rank0_g, rank1_g) in zip(at, wide):
                shared = (low_g & low) | (high_g & high)
                free = jnp.where(shared == 0, 1.0, 0.0).astype(jnp.bfloat16)
                for jj, step in enumerate((rank0 - rank0_g, rank1 - rank1_g)):
                    step = step.astype(jnp.bfloat16)
                    w[jj, pl.ds(a, 16), lanes] = jnp.minimum(jnp.maximum(step, -one), one) * free
        return 0

    lax.fori_loop(0, HP // BLOCK, payoff_rows, 0, unroll=2)

    for jj in range(2):
        wait_rows(arecv, (SECTIONS - 1) * TILES, a_rs.at[jj])
        reach = [end_of(0, jj), end_of(1, jj)]
        for s in range(SECTIONS):
            go = jnp.where(inside, unit(arecv, jj * SECTIONS + s)[...], 0.5)
            q = s % 2
            unit(lsc, (2 * jj + q) * SECTIONS + s)[...] = reach[q] * (1.0 - go)
            unit(lsc, (2 * jj + 1 - q) * SECTIONS + s)[...] = reach[1 - q]
            reach[q] = reach[q] * go
        for p in range(2):
            for t in range(TILES):
                tile = lsc[pl.ds((2 * jj + p) * SECTIONS * UNIT + t, SECTIONS, stride=UNIT), :]
                lhs[jj, p * SECTIONS : (p + 1) * SECTIONS, 128 * t : 128 * (t + 1)] = tile.astype(jnp.bfloat16)
        leaf = jnp.dot(lhs[jj], w[jj], preferred_element_type=jnp.float32)
        for p in range(2):
            for t in range(TILES):
                tile = leaf[p * SECTIONS : (p + 1) * SECTIONS, 128 * t : 128 * (t + 1)]
                leafsc[pl.ds((2 * jj + 1 - p) * SECTIONS * UNIT + t, SECTIONS, stride=UNIT), :] = tile

    value = [[end_of(2, jj), end_of(3, jj)] for jj in range(2)]
    for s in reversed(range(SECTIONS)):
        q = s % 2
        for jj in range(2):
            go = jnp.where(inside, unit(arecv, jj * SECTIONS + s)[...], 0.5)
            leaf_q = unit(leafsc, (2 * jj + q) * SECTIONS + s)[...] * mask[jj]
            leaf_o = unit(leafsc, (2 * jj + 1 - q) * SECTIONS + s)[...] * mask[jj]
            unit(gsend, jj * SECTIONS + s)[...] = leaf_q - value[jj][q]
            value[jj][q] = (1.0 - go) * leaf_q + go * value[jj][q]
            value[jj][1 - q] = leaf_o + value[jj][1 - q]
        for p in range(2):
            unit(rsend, 2 * s + p, HALF)[...] = sum(
                jnp.where(inside, value[jj][p], 1.0) * alive[jj] for jj in range(2)
            )

    def r_copy(dc, db):
        to_core = (core + dc) % 2
        to_col = column(db)
        to = 2 * node + to_core
        s = (to_col + 7 * to) % SECTIONS
        return remote(
            unit(rsend, 2 * s + to_core, HALF), unit(rrecv, dc * COLUMNS + db, HALF), r_ss, r_rs, to, to_col,
        )

    pairs = [(dc, db) for db in FAR for dc in range(2) if dc or db]
    for dc, db in pairs:
        r_copy(dc, db).start()

    def g_copy(jj, to):
        return remote(
            unit(gsend, jj * SECTIONS + to), unit(grecv, a_unit(jj, me)), g_ss, g_rs, to, col
        )

    for jj in range(2):
        for d in ORDER:
            g_copy(jj, (me + d) % SECTIONS).start()
    for jj in range(2):
        unit(grecv, a_unit(jj, me))[...] = unit(gsend, jj * SECTIONS + me)[...]

    mine = (col + 7 * me) % SECTIONS
    total = unit(rsend, 2 * mine + core, HALF)[...]
    wait_rows(rrecv, (2 * COLUMNS - 1) * TILES, r_rs)
    for dc, db in pairs:
        total = total + unit(rrecv, dc * COLUMNS + db, HALF)[...]
    fsend[:TILES, :] = total / total[TILES - 1 : TILES, 127:128]

    def f_copy(db):
        return remote(unit(fsend, 0), unit(frecv, me), f_ss, f_rs, mine, column(db))

    for db in FAR[:-1]:
        f_copy(db).start()

    @pl.when(mine != me)
    def _():
        f_copy(0).start()

    @pl.when(mine == me)
    def _():
        unit(frecv, me)[...] = fsend[:TILES, :]

    wait_rows(grecv, (SECTIONS - 1) * 2 * TILES, g_rs)
    for j in range(BOARD_DEV):
        keep = live_s[j] > 0
        for t in range(TILES):
            size = 128 if t < TILES - 1 else LAST
            at = pl.ds(128 * t, size)
            first = (j % 2 * 2 + j // 2) * NODES * UNIT
            gap = grecv[pl.ds(first + t, NODES, stride=UNIT), :][:, :size]
            stop = regret_v[0, j, :, at]
            go = regret_v[1, j, :, at]
            total_regret = stop + go
            out_stop[j, :, at] = jnp.where(keep, jnp.maximum(stop + go / total_regret * gap, 0.0), stop)
            out_go[j, :, at] = jnp.where(keep, jnp.maximum(go - stop / total_regret * gap, 0.0), go)

    wait_rows(asend, (SECTIONS - 1) * 2 * TILES, a_ss)
    wait_rows(gsend, (SECTIONS - 1) * 2 * TILES, g_ss)
    wait_rows(rsend, (2 * COLUMNS - 1) * TILES, r_ss)

    @pl.when(mine != me)
    def _():
        wait_rows(frecv, COLUMNS * TILES, f_ss)

    @pl.when(mine == me)
    def _():
        wait_rows(frecv, (COLUMNS - 1) * TILES, f_ss)

    @pl.when(mine != me)
    def _():
        wait_rows(frecv, SECTIONS * TILES, f_rs)

    @pl.when(mine == me)
    def _():
        wait_rows(frecv, (SECTIONS - 1) * TILES, f_rs)

    for p in range(2):
        for t in range(TILES):
            size = 128 if t < TILES - 1 else LAST
            tile = frecv[pl.ds(p * UNIT + t, NODES, stride=2 * UNIT), :]
            out_sec[p, :, pl.ds(128 * t, size)] = tile[:, :size]


def store(stop_v, go_v, sec_v, out_stop, out_go, out_sec, sem):
    pairs = ((stop_v, out_stop), (go_v, out_go), (sec_v, out_sec))
    copies = [pltpu.make_async_copy(src, dst.at[0], sem.at[i]) for i, (src, dst) in enumerate(pairs)]
    for copy in copies:
        copy.start()
    for copy in copies:
        copy.wait()


def local(root_reach, frontier_value, regret_stop, regret_go, board_live, board_cards, hand_rank):
    bits, scan = hand_bits()
    f32, i32 = jnp.float32, jnp.int32
    regrets = (BOARD_DEV, NODES, H)
    ends = (2, NODES, H)
    hbm_spec = pl.BlockSpec(memory_space=pltpu.HBM)
    vmem_spec = pl.BlockSpec(memory_space=pltpu.VMEM)
    dma = pltpu.SemaphoreType.DMA
    operands = (
        root_reach, frontier_value, regret_stop[0], regret_go[0], board_live, board_cards, hand_rank,
        jnp.asarray(bits), jnp.asarray(scan),
    )
    new_stop, new_go, section_value = pl.pallas_call(
        kernel,
        out_shape=(
            pltpu.VMEM(regrets, f32),
            pltpu.VMEM(regrets, f32),
            pltpu.VMEM(ends, f32),
        ),
        in_specs=[hbm_spec] * 9,
        out_specs=(vmem_spec,) * 3,
        scratch_shapes=[
            pltpu.VMEM(ends, f32), pltpu.VMEM(ends, f32), pltpu.VMEM((2, *regrets), f32),
            pltpu.SMEM((BOARD_DEV,), i32), pltpu.SMEM((BOARD_DEV, 5), i32), pltpu.VMEM((BOARD_DEV, H), i32),
            pltpu.VMEM((2, HP), i32), pltpu.VMEM((2, TILES, 128), i32),
            pltpu.VMEM((BOARD_DEV, NODES, 128), f32),
            pltpu.VMEM((2 * SECTIONS * UNIT, 128), f32), pltpu.VMEM((2 * SECTIONS * UNIT, 128), f32),
            pltpu.VMEM((4 * NODES * UNIT, 128), f32),
            pltpu.VMEM((8, HP), i32), pltpu.VMEM((8, HP), f32), pltpu.VMEM((2, 8, HP), i32), pltpu.VMEM((2, 8, HP), f32),
            pltpu.VMEM((HP, 8), i32), pltpu.VMEM((HP, 8), f32),
            pltpu.VMEM((2, HP, HP), jnp.bfloat16),
            pltpu.VMEM((4 * SECTIONS * UNIT, 128), f32), pltpu.VMEM((2, 2 * SECTIONS, HP), jnp.bfloat16),
            pltpu.VMEM((4 * SECTIONS * UNIT, 128), f32),
            pltpu.VMEM((2 * SECTIONS * UNIT, 128), f32), pltpu.VMEM((2 * SECTIONS * UNIT, 128), f32),
            pltpu.VMEM((2 * SECTIONS * HALF, 128), f32), pltpu.VMEM((2 * COLUMNS * HALF, 128), f32),
            pltpu.VMEM((HALF, 128), f32), pltpu.VMEM((SECTIONS * UNIT, 128), f32),
            dma((7,)), dma, dma, dma((2,)), *([dma] * 6),
        ],
        compiler_params=pltpu.CompilerParams(
            collective_id=0, has_side_effects=True, vmem_limit_bytes=32 * 1024 * 1024
        ),
    )(*(pltpu.with_memory_space_constraint(x, pltpu.HBM) for x in operands))
    return pl.pallas_call(
        store,
        out_shape=(
            jax.ShapeDtypeStruct((1, *regrets), f32),
            jax.ShapeDtypeStruct((1, *regrets), f32),
            jax.ShapeDtypeStruct((1, *ends), f32),
        ),
        in_specs=[vmem_spec] * 3,
        out_specs=(hbm_spec,) * 3,
        scratch_shapes=[dma((3,))],
        compiler_params=pltpu.CompilerParams(vmem_limit_bytes=1024 * 1024),
    )(new_stop, new_go, section_value)


def solution(mesh):
    regrets = P("section", "board", None, None)
    return jax.shard_map(
        local,
        mesh=mesh,
        in_specs=(P(), P(), regrets, regrets, P("board"), P("board", None), P("board", None)),
        out_specs=(regrets, regrets, P("section", None, None, None)),
        check_vma=False,
    )
```

time: 33.6 us -> 31.6 us (0.940)
  Pallas kernels: 32.8 us -> 30.9 us
    pallas_call x1, Pallas kernels: 32.1 us -> 30.1 us  [local(): pl.pallas_call(kernel, out_shape=(pltpu.VMEM(regrets, f32), pltpu.VMEM(re...]
where the time goes in v4:
time: 31.6 us; the launch traced here: 31.5 us
  Pallas kernels  30.9 us (98%)
  between operations  0.64 us (2%)
    pallas_call x1, Pallas kernels, local(): pl.pallas_call(kernel, out_shape=(pltpu.VMEM(regrets, f32), pltpu.VMEM(re...  30.1 us
    pallas_call x1, Pallas kernels, local(): pl.pallas_call(store, out_shape=(jax.ShapeDtypeStruct((1, *regrets), f32)...  0.79 us

profile of v4, /device:TPU:1, one launch (start us, length us, event | category | flops | bytes accessed | tf_op | source)
XLA Modules:
  0.0 31.5 jit_solution(13156830319221325294)
XLA Ops:
  0.6 30.1 %shard_map.112 = (f32[4,8,1326]{2,1,0:T(8,128)S(1)}, f32[4,8,1326]{2,1,0:T(8,128)S(1)}, f32[2,8,1326]{2,1,0:T(8,128)S(1)}) custom-call(f32[2,8,1326]{2,1,0:T(8,128)} %root_hbm.1, f32[2,8,1326]{2,1,0:T(8,128)} %front_hbm.1, f32[4,8,1326]{2,1,0:T(8,128)} %bitcast.2, f32[4,8,1326]{2,1,0:T(8,128)} %bitcast.3, s32[4]{0:T(128)} %live_hbm.1, s32[4,5]{1,0:T(4,128)} %cards_hbm.1, ...), custom_call_target="tpu_custom_call" | custom-call | tf_op jit(solution)/shard_map/pallas_call | solution.py:339
  30.7 0.8 %shard_map.113 = (f32[1,4,8,1326]{3,2,1,0:T(8,128)}, f32[1,4,8,1326]{3,2,1,0:T(8,128)}, f32[1,2,8,1326]{3,2,1,0:T(8,128)}) custom-call(f32[4,8,1326]{2,1,0:T(8,128)S(1)} %get-tuple-element.6.stop_v, f32[4,8,1326]{2,1,0:T(8,128)S(1)} %get-tuple-element.7.go_v, f32[2,8,1326]{2,1,0:T(8,128)S(1)} %get-tuple-element.8.sec_v), custom_call_target="tpu_custom_call" | custom-call | tf_op jit(solution)/shard_map/pallas_call | solution.py:369

commit v5 on v4

--- a/solution.py
+++ b/solution.py
@@ -16,10 +16,13 @@
 COLUMNS = 16
 BOARD_DEV = 4
 UNIT = 24
-BLOCK = 32
+BLOCK = 64
+AHEAD = 2
 HALF = 16
 MESH = pl.DeviceIdType.MESH
 ORDER = sorted(range(1, SECTIONS), key=lambda d: -min(d, SECTIONS - d))
+EARLY_SECTIONS = (0, 1, 2, 3, 4, 5, 6, 7, 10, 11, 12, 13, 14, 15, 8, 9)
+EARLY_COLUMNS = (0, 1, 3, 4, 2, 8, 5, 12, 7, 9, 6, 13, 11, 15, 10, 14)
 FAR = sorted(range(COLUMNS), key=lambda d: -min(d // 4, 4 - d // 4) - min(d % 4, 4 - d % 4))
 
 
@@ -71,6 +74,13 @@
     def column(db):
         return (row + db // 4) % 4 * 4 + (lane + db % 4) % 4
 
+    barrier = pltpu.get_barrier_semaphore()
+
+    def greet(section, board):
+        pl.semaphore_signal(barrier, inc=1, device_id={"section": section, "board": board}, device_id_type=MESH)
+
+    for d in ORDER:
+        greet((me + d) % SECTIONS, col)
     loads = [
         pltpu.make_async_copy(src, dst, in_sem.at[i])
         for i, (src, dst) in enumerate(
@@ -85,13 +95,6 @@
         pltpu.make_async_copy(src, regret_v.at[i], regret_sem).start()
     for copy in loads:
         copy.start()
-    barrier = pltpu.get_barrier_semaphore()
-
-    def greet(section, board):
-        pl.semaphore_signal(barrier, inc=1, device_id={"section": section, "board": board}, device_id_type=MESH)
-
-    for d in ORDER:
-        greet((me + d) % SECTIONS, col)
     for db in FAR[:-1]:
         for dc in range(2):
             greet(2 * node + (core + dc) % 2, column(db))
@@ -156,22 +159,6 @@
         lanes = slice(128 * t, 128 * (t + 1))
         bitcol[lanes, :] = bitrow[:, lanes].T
         rankcol[lanes, :] = rankrow[:, lanes].T
-
-    pl.semaphore_wait(barrier, SECTIONS - 1 + 2 * (COLUMNS - 1))
-
-    def a_unit(jj, to):
-        return (2 * jj + to % 2) * NODES + to // 2
-
-    def a_copy(jj, to):
-        return remote(
-            unit(asend, a_unit(jj, to)), unit(arecv, jj * SECTIONS + me), a_ss, a_rs.at[jj], to, col
-        )
-
-    for jj in range(2):
-        for d in ORDER:
-            a_copy(jj, (me + d) % SECTIONS).start()
-    for jj in range(2):
-        unit(arecv, jj * SECTIONS + me)[...] = unit(asend, a_unit(jj, me))[...]
 
     def payoff_rows(block, _):
         at = [pl.multiple_of(block * BLOCK + 16 * i, 16) for i in range(BLOCK // 16)]
@@ -193,7 +180,24 @@
                     w[jj, pl.ds(a, 16), lanes] = jnp.minimum(jnp.maximum(step, -one), one) * free
         return 0
 
-    lax.fori_loop(0, HP // BLOCK, payoff_rows, 0, unroll=2)
+    lax.fori_loop(0, AHEAD, payoff_rows, 0)
+    pl.semaphore_wait(barrier, SECTIONS - 1 + 2 * (COLUMNS - 1))
+
+    def a_unit(jj, to):
+        return (2 * jj + to % 2) * NODES + to // 2
+
+    def a_copy(jj, to):
+        return remote(
+            unit(asend, a_unit(jj, to)), unit(arecv, jj * SECTIONS + me), a_ss, a_rs.at[jj], to, col
+        )
+
+    for jj in range(2):
+        for d in ORDER:
+            a_copy(jj, (me + d) % SECTIONS).start()
+    for jj in range(2):
+        unit(arecv, jj * SECTIONS + me)[...] = unit(asend, a_unit(jj, me))[...]
+
+    lax.fori_loop(AHEAD, HP // BLOCK, payoff_rows, 0)
 
     for jj in range(2):
         wait_rows(arecv, (SECTIONS - 1) * TILES, a_rs.at[jj])
@@ -229,18 +233,22 @@
                 jnp.where(inside, value[jj][p], 1.0) * alive[jj] for jj in range(2)
             )
 
-    def r_copy(dc, db):
-        to_core = (core + dc) % 2
-        to_col = column(db)
-        to = 2 * node + to_core
-        s = (to_col + 7 * to) % SECTIONS
+    mine = (col + 7 * me) % SECTIONS
+
+    def r_copy(s, p):
+        to = 2 * node + p
         return remote(
-            unit(rsend, 2 * s + to_core, HALF), unit(rrecv, dc * COLUMNS + db, HALF), r_ss, r_rs, to, to_col,
+            unit(rsend, 2 * s + p, HALF), unit(rrecv, core * COLUMNS + col, HALF), r_ss, r_rs,
+            to, (s + (SECTIONS - 7) * to) % COLUMNS,
         )
 
-    pairs = [(dc, db) for db in FAR for dc in range(2) if dc or db]
-    for dc, db in pairs:
-        r_copy(dc, db).start()
+    for s in EARLY_SECTIONS:
+        for p in range(2):
+            @pl.when(jnp.logical_or(core != p, mine != s))
+            def _(s=s, p=p):
+                r_copy(s, p).start()
+
+    unit(rrecv, core * COLUMNS + col, HALF)[...] = unit(rsend, 2 * mine + core, HALF)[...]
 
     def g_copy(jj, to):
         return remote(
@@ -253,22 +261,19 @@
     for jj in range(2):
         unit(grecv, a_unit(jj, me))[...] = unit(gsend, jj * SECTIONS + me)[...]
 
-    mine = (col + 7 * me) % SECTIONS
-    total = unit(rsend, 2 * mine + core, HALF)[...]
     wait_rows(rrecv, (2 * COLUMNS - 1) * TILES, r_rs)
-    for dc, db in pairs:
-        total = total + unit(rrecv, dc * COLUMNS + db, HALF)[...]
+    total = unit(rrecv, 0, HALF)[...]
+    for k in range(1, 2 * COLUMNS):
+        total = total + unit(rrecv, k, HALF)[...]
     fsend[:TILES, :] = total / total[TILES - 1 : TILES, 127:128]
 
-    def f_copy(db):
-        return remote(unit(fsend, 0), unit(frecv, me), f_ss, f_rs, mine, column(db))
-
-    for db in FAR[:-1]:
-        f_copy(db).start()
-
-    @pl.when(mine != me)
-    def _():
-        f_copy(0).start()
+    def f_copy(to_col):
+        return remote(unit(fsend, 0), unit(frecv, me), f_ss, f_rs, mine, to_col)
+
+    for to_col in EARLY_COLUMNS:
+        @pl.when(jnp.logical_or(mine != me, col != to_col))
+        def _(to_col=to_col):
+            f_copy(to_col).start()
 
     @pl.when(mine == me)
     def _():

time: 31.6 us -> 30.9 us (0.978)
  Pallas kernels: 30.9 us -> 30.1 us
    pallas_call x1, Pallas kernels: 30.1 us -> 29.3 us  [local(): pl.pallas_call(kernel, out_shape=(pltpu.VMEM(regrets, f32), pltpu.VMEM(re...]
where the time goes in v5:
time: 30.9 us; the launch traced here: 30.8 us
  Pallas kernels  30.1 us (97%)
  between operations  0.64 us (2%)
    pallas_call x1, Pallas kernels, local(): pl.pallas_call(kernel, out_shape=(pltpu.VMEM(regrets, f32), pltpu.VMEM(re...  29.3 us
    pallas_call x1, Pallas kernels, local(): pl.pallas_call(store, out_shape=(jax.ShapeDtypeStruct((1, *regrets), f32)...  0.79 us

profile of v5, /device:TPU:1, one launch (start us, length us, event | category | flops | bytes accessed | tf_op | source)
XLA Modules:
  0.0 30.8 jit_solution(1249556517972027728)
XLA Ops:
  0.6 29.3 %shard_map.112 = (f32[4,8,1326]{2,1,0:T(8,128)S(1)}, f32[4,8,1326]{2,1,0:T(8,128)S(1)}, f32[2,8,1326]{2,1,0:T(8,128)S(1)}) custom-call(f32[2,8,1326]{2,1,0:T(8,128)} %root_hbm.1, f32[2,8,1326]{2,1,0:T(8,128)} %front_hbm.1, f32[4,8,1326]{2,1,0:T(8,128)} %bitcast.2, f32[4,8,1326]{2,1,0:T(8,128)} %bitcast.3, s32[4]{0:T(128)} %live_hbm.1, s32[4,5]{1,0:T(4,128)} %cards_hbm.1, ...), custom_call_target="tpu_custom_call" | custom-call | tf_op jit(solution)/shard_map/pallas_call | solution.py:344
  30.0 0.8 %shard_map.113 = (f32[1,4,8,1326]{3,2,1,0:T(8,128)}, f32[1,4,8,1326]{3,2,1,0:T(8,128)}, f32[1,2,8,1326]{3,2,1,0:T(8,128)}) custom-call(f32[4,8,1326]{2,1,0:T(8,128)S(1)} %get-tuple-element.6.stop_v, f32[4,8,1326]{2,1,0:T(8,128)S(1)} %get-tuple-element.7.go_v, f32[2,8,1326]{2,1,0:T(8,128)S(1)} %get-tuple-element.8.sec_v), custom_call_target="tpu_custom_call" | custom-call | tf_op jit(solution)/shard_map/pallas_call | solution.py:374

commit v6 on v5

--- a/solution.py
+++ b/solution.py
@@ -21,7 +21,7 @@
 HALF = 16
 MESH = pl.DeviceIdType.MESH
 ORDER = sorted(range(1, SECTIONS), key=lambda d: -min(d, SECTIONS - d))
-EARLY_SECTIONS = (0, 1, 2, 3, 4, 5, 6, 7, 10, 11, 12, 13, 14, 15, 8, 9)
+EARLY_SECTIONS = (1, 3, 2, 0, 5, 4, 7, 6, 10, 11, 12, 13, 14, 15, 8, 9)
 EARLY_COLUMNS = (0, 1, 3, 4, 2, 8, 5, 12, 7, 9, 6, 13, 11, 15, 10, 14)
 FAR = sorted(range(COLUMNS), key=lambda d: -min(d // 4, 4 - d // 4) - min(d % 4, 4 - d % 4))
 
@@ -74,6 +74,9 @@
     def column(db):
         return (row + db // 4) % 4 * 4 + (lane + db % 4) % 4
 
+    for i, src in enumerate((stop_hbm, go_hbm)):
+        pltpu.make_async_copy(src, regret_v.at[i], regret_sem).start()
+
     barrier = pltpu.get_barrier_semaphore()
 
     def greet(section, board):
@@ -91,8 +94,6 @@
             ]
         )
     ]
-    for i, src in enumerate((stop_hbm, go_hbm)):
-        pltpu.make_async_copy(src, regret_v.at[i], regret_sem).start()
     for copy in loads:
         copy.start()
     for db in FAR[:-1]:
@@ -225,7 +226,7 @@
             go = jnp.where(inside, unit(arecv, jj * SECTIONS + s)[...], 0.5)
             leaf_q = unit(leafsc, (2 * jj + q) * SECTIONS + s)[...] * mask[jj]
             leaf_o = unit(leafsc, (2 * jj + 1 - q) * SECTIONS + s)[...] * mask[jj]
-            unit(gsend, jj * SECTIONS + s)[...] = leaf_q - value[jj][q]
+            gsend[s * UNIT + jj * TILES : s * UNIT + (jj + 1) * TILES, :] = leaf_q - value[jj][q]
             value[jj][q] = (1.0 - go) * leaf_q + go * value[jj][q]
             value[jj][1 - q] = leaf_o + value[jj][1 - q]
         for p in range(2):
@@ -250,21 +251,24 @@
 
     unit(rrecv, core * COLUMNS + col, HALF)[...] = unit(rsend, 2 * mine + core, HALF)[...]
 
-    def g_copy(jj, to):
-        return remote(
-            unit(gsend, jj * SECTIONS + to), unit(grecv, a_unit(jj, me)), g_ss, g_rs, to, col
-        )
-
-    for jj in range(2):
-        for d in ORDER:
-            g_copy(jj, (me + d) % SECTIONS).start()
-    for jj in range(2):
-        unit(grecv, a_unit(jj, me))[...] = unit(gsend, jj * SECTIONS + me)[...]
+    def block(ref, index):
+        return ref.at[pl.ds(pl.multiple_of(index * UNIT, 8), 2 * TILES), :]
+
+    def place(to):
+        return to % 2 * NODES + to // 2
+
+    def g_copy(to):
+        return remote(block(gsend, to), block(grecv, place(me)), g_ss, g_rs, to, col)
+
+    for d in ORDER:
+        g_copy((me + d) % SECTIONS).start()
+    block(grecv, place(me))[...] = block(gsend, me)[...]
 
     wait_rows(rrecv, (2 * COLUMNS - 1) * TILES, r_rs)
-    total = unit(rrecv, 0, HALF)[...]
-    for k in range(1, 2 * COLUMNS):
-        total = total + unit(rrecv, k, HALF)[...]
+    sums = [unit(rrecv, k, HALF)[...] for k in range(4)]
+    for k in range(4, 2 * COLUMNS):
+        sums[k % 4] = sums[k % 4] + unit(rrecv, k, HALF)[...]
+    total = (sums[0] + sums[1]) + (sums[2] + sums[3])
     fsend[:TILES, :] = total / total[TILES - 1 : TILES, 127:128]
 
     def f_copy(to_col):
@@ -285,7 +289,7 @@
         for t in range(TILES):
             size = 128 if t < TILES - 1 else LAST
             at = pl.ds(128 * t, size)
-            first = (j % 2 * 2 + j // 2) * NODES * UNIT
+            first = j // 2 * NODES * UNIT + j % 2 * TILES
             gap = grecv[pl.ds(first + t, NODES, stride=UNIT), :][:, :size]
             stop = regret_v[0, j, :, at]
             go = regret_v[1, j, :, at]
@@ -362,7 +366,7 @@
             pltpu.VMEM((2, HP, HP), jnp.bfloat16),
             pltpu.VMEM((4 * SECTIONS * UNIT, 128), f32), pltpu.VMEM((2, 2 * SECTIONS, HP), jnp.bfloat16),
             pltpu.VMEM((4 * SECTIONS * UNIT, 128), f32),
-            pltpu.VMEM((2 * SECTIONS * UNIT, 128), f32), pltpu.VMEM((2 * SECTIONS * UNIT, 128), f32),
+            pltpu.VMEM((SECTIONS * UNIT, 128), f32), pltpu.VMEM((SECTIONS * UNIT, 128), f32),
             pltpu.VMEM((2 * SECTIONS * HALF, 128), f32), pltpu.VMEM((2 * COLUMNS * HALF, 128), f32),
             pltpu.VMEM((HALF, 128), f32), pltpu.VMEM((SECTIONS * UNIT, 128), f32),
             dma((7,)), dma, dma, dma((2,)), *([dma] * 6),

time: 30.9 us -> 30.9 us (level)
  no operation moved by 1% of the time
where the time goes in v6:
time: 30.9 us; the launch traced here: 30.7 us
  Pallas kernels  30.1 us (97%)
  between operations  0.64 us (2%)
    pallas_call x1, Pallas kernels, local(): pl.pallas_call(kernel, out_shape=(pltpu.VMEM(regrets, f32), pltpu.VMEM(re...  29.3 us
    pallas_call x1, Pallas kernels, local(): pl.pallas_call(store, out_shape=(jax.ShapeDtypeStruct((1, *regrets), f32)...  0.79 us

profile of v6, /device:TPU:1, one launch (start us, length us, event | category | flops | bytes accessed | tf_op | source)
XLA Modules:
  0.0 30.7 jit_solution(5641148629132637579)
XLA Ops:
  0.6 29.3 %shard_map.112 = (f32[4,8,1326]{2,1,0:T(8,128)S(1)}, f32[4,8,1326]{2,1,0:T(8,128)S(1)}, f32[2,8,1326]{2,1,0:T(8,128)S(1)}) custom-call(f32[2,8,1326]{2,1,0:T(8,128)} %root_hbm.1, f32[2,8,1326]{2,1,0:T(8,128)} %front_hbm.1, f32[4,8,1326]{2,1,0:T(8,128)} %bitcast.2, f32[4,8,1326]{2,1,0:T(8,128)} %bitcast.3, s32[4]{0:T(128)} %live_hbm.1, s32[4,5]{1,0:T(4,128)} %cards_hbm.1, ...), custom_call_target="tpu_custom_call" | custom-call | tf_op jit(solution)/shard_map/pallas_call | solution.py:348
  30.0 0.8 %shard_map.113 = (f32[1,4,8,1326]{3,2,1,0:T(8,128)}, f32[1,4,8,1326]{3,2,1,0:T(8,128)}, f32[1,2,8,1326]{3,2,1,0:T(8,128)}) custom-call(f32[4,8,1326]{2,1,0:T(8,128)S(1)} %get-tuple-element.6.stop_v, f32[4,8,1326]{2,1,0:T(8,128)S(1)} %get-tuple-element.7.go_v, f32[2,8,1326]{2,1,0:T(8,128)S(1)} %get-tuple-element.8.sec_v), custom_call_target="tpu_custom_call" | custom-call | tf_op jit(solution)/shard_map/pallas_call | solution.py:378

commit v7 on v6

--- a/solution.py
+++ b/solution.py
@@ -218,21 +218,19 @@
             for t in range(TILES):
                 tile = leaf[p * SECTIONS : (p + 1) * SECTIONS, 128 * t : 128 * (t + 1)]
                 leafsc[pl.ds((2 * jj + 1 - p) * SECTIONS * UNIT + t, SECTIONS, stride=UNIT), :] = tile
-
-    value = [[end_of(2, jj), end_of(3, jj)] for jj in range(2)]
-    for s in reversed(range(SECTIONS)):
-        q = s % 2
-        for jj in range(2):
+        value = [end_of(2, jj), end_of(3, jj)]
+        for s in reversed(range(SECTIONS)):
+            q = s % 2
             go = jnp.where(inside, unit(arecv, jj * SECTIONS + s)[...], 0.5)
             leaf_q = unit(leafsc, (2 * jj + q) * SECTIONS + s)[...] * mask[jj]
             leaf_o = unit(leafsc, (2 * jj + 1 - q) * SECTIONS + s)[...] * mask[jj]
-            gsend[s * UNIT + jj * TILES : s * UNIT + (jj + 1) * TILES, :] = leaf_q - value[jj][q]
-            value[jj][q] = (1.0 - go) * leaf_q + go * value[jj][q]
-            value[jj][1 - q] = leaf_o + value[jj][1 - q]
-        for p in range(2):
-            unit(rsend, 2 * s + p, HALF)[...] = sum(
-                jnp.where(inside, value[jj][p], 1.0) * alive[jj] for jj in range(2)
-            )
+            gsend[s * UNIT + jj * TILES : s * UNIT + (jj + 1) * TILES, :] = leaf_q - value[q]
+            value[q] = (1.0 - go) * leaf_q + go * value[q]
+            value[1 - q] = leaf_o + value[1 - q]
+            for p in range(2):
+                row = unit(rsend, 2 * s + p, HALF)
+                part = jnp.where(inside, value[p], 1.0) * alive[jj]
+                row[...] = part if jj == 0 else row[...] + part
 
     mine = (col + 7 * me) % SECTIONS
 

time: 30.9 us -> 30.8 us (level)
  no operation moved by 1% of the time
where the time goes in v7:
time: 30.8 us; the launch traced here: 30.7 us
  Pallas kernels  30.1 us (98%)
  between operations  0.64 us (2%)
    pallas_call x1, Pallas kernels, local(): pl.pallas_call(kernel, out_shape=(pltpu.VMEM(regrets, f32), pltpu.VMEM(re...  29.3 us
    pallas_call x1, Pallas kernels, local(): pl.pallas_call(store, out_shape=(jax.ShapeDtypeStruct((1, *regrets), f32)...  0.79 us

profile of v7, /device:TPU:1, one launch (start us, length us, event | category | flops | bytes accessed | tf_op | source)
XLA Modules:
  0.0 30.7 jit_solution(1533279589120152146)
XLA Ops:
  0.6 29.3 %shard_map.112 = (f32[4,8,1326]{2,1,0:T(8,128)S(1)}, f32[4,8,1326]{2,1,0:T(8,128)S(1)}, f32[2,8,1326]{2,1,0:T(8,128)S(1)}) custom-call(f32[2,8,1326]{2,1,0:T(8,128)} %root_hbm.1, f32[2,8,1326]{2,1,0:T(8,128)} %front_hbm.1, f32[4,8,1326]{2,1,0:T(8,128)} %bitcast.2, f32[4,8,1326]{2,1,0:T(8,128)} %bitcast.3, s32[4]{0:T(128)} %live_hbm.1, s32[4,5]{1,0:T(4,128)} %cards_hbm.1, ...), custom_call_target="tpu_custom_call" | custom-call | tf_op jit(solution)/shard_map/pallas_call | solution.py:346
  30.0 0.8 %shard_map.113 = (f32[1,4,8,1326]{3,2,1,0:T(8,128)}, f32[1,4,8,1326]{3,2,1,0:T(8,128)}, f32[1,2,8,1326]{3,2,1,0:T(8,128)}) custom-call(f32[4,8,1326]{2,1,0:T(8,128)S(1)} %get-tuple-element.6.stop_v, f32[4,8,1326]{2,1,0:T(8,128)S(1)} %get-tuple-element.7.go_v, f32[2,8,1326]{2,1,0:T(8,128)S(1)} %get-tuple-element.8.sec_v), custom_call_target="tpu_custom_call" | custom-call | tf_op jit(solution)/shard_map/pallas_call | solution.py:376

commit v8 on v7

--- a/solution.py
+++ b/solution.py
@@ -23,7 +23,11 @@
 ORDER = sorted(range(1, SECTIONS), key=lambda d: -min(d, SECTIONS - d))
 EARLY_SECTIONS = (1, 3, 2, 0, 5, 4, 7, 6, 10, 11, 12, 13, 14, 15, 8, 9)
 EARLY_COLUMNS = (0, 1, 3, 4, 2, 8, 5, 12, 7, 9, 6, 13, 11, 15, 10, 14)
-FAR = sorted(range(COLUMNS), key=lambda d: -min(d // 4, 4 - d // 4) - min(d % 4, 4 - d % 4))
+def far_of(d):
+    return min(d // 4, 4 - d // 4) + min(d % 4, 4 - d % 4)
+
+
+FAR = sorted(range(COLUMNS), key=lambda d: -far_of(d))
 
 
 def hand_bits():
@@ -82,8 +86,17 @@
     def greet(section, board):
         pl.semaphore_signal(barrier, inc=1, device_id={"section": section, "board": board}, device_id_type=MESH)
 
-    for d in ORDER:
-        greet((me + d) % SECTIONS, col)
+    def greet_all(near):
+        for hops in (2, 1, 0) if near else (4, 3):
+            for d in ORDER:
+                if (min(d, SECTIONS - d) + 1) // 2 == hops or (hops == 0 and d == 0):
+                    greet((me + d) % SECTIONS, col)
+            for db in FAR[:-1]:
+                if far_of(db) == hops:
+                    for dc in range(2):
+                        greet(2 * node + (core + dc) % 2, column(db))
+
+    greet_all(False)
     loads = [
         pltpu.make_async_copy(src, dst, in_sem.at[i])
         for i, (src, dst) in enumerate(
@@ -96,9 +109,7 @@
     ]
     for copy in loads:
         copy.start()
-    for db in FAR[:-1]:
-        for dc in range(2):
-            greet(2 * node + (core + dc) % 2, column(db))
+    greet_all(True)
     pad[...] = jnp.full(pad.shape, 0.5, jnp.float32)
     ends[...] = jnp.zeros(ends.shape, jnp.float32)
     pltpu.make_async_copy(regret_v, regret_v, regret_sem).wait()

time: 30.8 us -> 30.8 us (level)
  no operation moved by 1% of the time
where the time goes in v8:
time: 30.8 us; the launch traced here: 30.7 us
  Pallas kernels  30 us (97%)
  between operations  0.64 us (2%)
    pallas_call x1, Pallas kernels, local(): pl.pallas_call(kernel, out_shape=(pltpu.VMEM(regrets, f32), pltpu.VMEM(re...  29.2 us
    pallas_call x1, Pallas kernels, local(): pl.pallas_call(store, out_shape=(jax.ShapeDtypeStruct((1, *regrets), f32)...  0.79 us

profile of v8, /device:TPU:1, one launch (start us, length us, event | category | flops | bytes accessed | tf_op | source)
XLA Modules:
  0.0 30.7 jit_solution(8597952556014741336)
XLA Ops:
  0.6 29.2 %shard_map.112 = (f32[4,8,1326]{2,1,0:T(8,128)S(1)}, f32[4,8,1326]{2,1,0:T(8,128)S(1)}, f32[2,8,1326]{2,1,0:T(8,128)S(1)}) custom-call(f32[2,8,1326]{2,1,0:T(8,128)} %root_hbm.1, f32[2,8,1326]{2,1,0:T(8,128)} %front_hbm.1, f32[4,8,1326]{2,1,0:T(8,128)} %bitcast.2, f32[4,8,1326]{2,1,0:T(8,128)} %bitcast.3, s32[4]{0:T(128)} %live_hbm.1, s32[4,5]{1,0:T(4,128)} %cards_hbm.1, ...), custom_call_target="tpu_custom_call" | custom-call | tf_op jit(solution)/shard_map/pallas_call | solution.py:357
  29.9 0.8 %shard_map.113 = (f32[1,4,8,1326]{3,2,1,0:T(8,128)}, f32[1,4,8,1326]{3,2,1,0:T(8,128)}, f32[1,2,8,1326]{3,2,1,0:T(8,128)}) custom-call(f32[4,8,1326]{2,1,0:T(8,128)S(1)} %get-tuple-element.6.stop_v, f32[4,8,1326]{2,1,0:T(8,128)S(1)} %get-tuple-element.7.go_v, f32[2,8,1326]{2,1,0:T(8,128)S(1)} %get-tuple-element.8.sec_v), custom_call_target="tpu_custom_call" | custom-call | tf_op jit(solution)/shard_map/pallas_call | solution.py:387
